TPU v7x, 16 devices: a whole 2x2x2 slice. The times are simulated.
16 devices in a mesh: dp: 1, tp: 16 (over x, y, z, core).
Axes of the slice: x: 2, y: 2, z: 2, core: 2. Of those that a mesh axis runs over, the one named last changes fastest.
Arguments:
- x: bfloat16 [4096, 4608], P(('dp', 'tp'))
- w_gate: bfloat16 [4608, 36864], P(None, 'tp')
- w_up: bfloat16 [4608, 36864], P(None, 'tp')
- w_down: bfloat16 [36864, 4608], P('tp')
Outputs:
- output: bfloat16 [4096, 4608], P(('dp', 'tp'))
All inputs are finite; a program needn't handle non-finite values.
Results may differ from a plain program's by a relative error of at most 0.016.
Values are sent between devices in bfloat16 or wider.
A program may use at most 2 GiB of HBM per device.

v0:
```python
import jax
import jax.numpy as jnp
from jax import lax
from jax.sharding import PartitionSpec as P


def solution(mesh):
    def step(x, w_gate, w_up, w_down):
        rows = lax.all_gather(x, "tp", axis=0, tiled=True)
        gate = jnp.dot(rows, w_gate, preferred_element_type=jnp.float32)
        up = jnp.dot(rows, w_up, preferred_element_type=jnp.float32)
        hidden = (jax.nn.gelu(gate) * up).astype(jnp.bfloat16)
        term = jnp.dot(hidden, w_down, preferred_element_type=jnp.float32).astype(jnp.bfloat16)
        return lax.psum_scatter(term, "tp", scatter_dimension=0, tiled=True)

    return jax.shard_map(
        step,
        mesh=mesh,
        in_specs=(P(("dp", "tp"), None), P(None, "tp"), P(None, "tp"), P("tp", None)),
        out_specs=P(("dp", "tp"), None),
        check_vma=False,
    )
```

profile of v0, /device:TPU:0, one launch (start us, length us, event | category | flops | bytes accessed | tf_op | source)
XLA Modules:
  0.0 666.4 jit_solution(11829898030020331532)
XLA Ops:
  6.5 0.0 all-gather.2.cloned.1.call-start
  6.5 0.7 all-gather.2.cloned.1.call-update
  7.3 0.0 reduce-scatter.2.cloned.1.call-start
  7.3 150.1 %all-gather.2.cloned.1.call-done = bf16[4096,4608]{1,0:T(8,128)(2,1)} async-done(((bf16[256,4608]{1,0:T(8,128)(2,1)}), bf16[4096,4608]{1,0:T(8,128)(2,1)}) %all-gather.2.cloned.1.call-update) | async-done | bytes 37748752 | tf_op jit(solution)/shard_map/all_gather | solution.py:9
  157.4 99.5 %fusion.9 = f32[4096,2304]{1,0:T(8,128)} fusion(bf16[4096,4608]{1,0:T(8,128)(2,1)} %all-gather.2.cloned.1.call-done, bf16[4608,2304]{1,0:T(8,128)(2,1)} %param.5), kind=kOutput, calls=%fused_computation.11 | convolution fusion | flops 86973087744 | bytes 96731136 | tf_op jit(solution)/shard_map/dot_general | solution.py:10
  256.9 103.8 %fusion.8 = bf16[4096,2304]{1,0:T(8,128)(2,1)} fusion(f32[4096,2304]{1,0:T(8,128)} %fusion.9, bf16[4096,4608]{1,0:T(8,128)(2,1)} %all-gather.2.cloned.1.call-done, bf16[4608,2304]{1,0:T(8,128)(2,1)} %param.6), kind=kOutput, calls=%fused_computation.10 | convolution fusion | flops 87067459584 | bytes 115605504 | tf_op jit(solution)/shard_map/dot_general | solution.py:11
  360.7 96.7 %convolution_convert_fusion = bf16[4096,4608]{1,0:T(8,128)(2,1)} fusion(bf16[4096,2304]{1,0:T(8,128)(2,1)} %fusion.8, bf16[2304,4608]{1,0:T(8,128)(2,1)} %param.7), kind=kOutput, calls=%fused_computation.1 | convolution fusion | flops 86991962112 | bytes 77856768 | tf_op jit(solution)/shard_map/dot_general | solution.py:13
  457.4 0.0 reduce-scatter.2.cloned.1.call-update
  457.5 202.1 %reduce-scatter.2.cloned.1.call-done = bf16[256,4608]{1,0:T(8,128)(2,1)} async-done(((bf16[4096,4608]{1,0:T(8,128)(2,1)}), bf16[256,4608]{1,0:T(8,128)(2,1)}) %reduce-scatter.2.cloned.1.call-update) | async-done | bytes 2359312 | tf_op jit(solution)/shard_map/reduce_scatter | solution.py:14
Async XLA Ops:
  6.5 150.8 %all-gather.2.cloned.1.call-start = ((), (), s32[]{:S(2)}) async-start(), calls=%async_computation.1 | async-start | bytes 40108032 | tf_op jit(solution)/shard_map/all_gather | solution.py:9
  7.3 652.3 %reduce-scatter.2.cloned.1.call-start = ((), (), s32[]{:S(2)}) async-start(), calls=%async_computation.2 | async-start | bytes 40108032 | tf_op jit(solution)/shard_map/reduce_scatter | solution.py:14
Sparse Core Ops, SparseCore 0:
  9.6 147.7 all-gather.1
  457.6 201.9 reduce-scatter.1
where the time goes:
time: 667 us; the launch traced here: 666 us
  waiting for transfers between devices  353 us (53%)
  matrix products  300 us (45%)
  between operations  13.4 us (2%)
    reduce_scatter x1, waiting for transfers between devices, step(): return lax.psum_scatter(term, 'tp', scatter_dimension=0, tiled=True)  202 us
    all_gather x1, waiting for transfers between devices, step(): rows = lax.all_gather(x, 'tp', axis=0, tiled=True)  150 us
    dot_general x1, matrix products, step(): up = jnp.dot(rows, w_up, preferred_element_type=jnp.float32)  104 us
    dot_general x1, matrix products, step(): gate = jnp.dot(rows, w_gate, preferred_element_type=jnp.float32)  99.5 us
    dot_general x1, matrix products, step(): jnp.dot(hidden, w_down, preferred_element_type=jnp.float32)  96.7 us
  transfers between devices with their start and end apart: 2, of which 2 were waited for; matrix products, arithmetic and copies ran while one was open for 0% of the time, Pallas kernels for 0%

commit v1 on v0

v1 whole, which is shorter than its diff:
```python
import functools

import jax
import jax.numpy as jnp
from jax import lax
from jax.experimental import pallas as pl
from jax.experimental.pallas import tpu as pltpu
from jax.sharding import PartitionSpec as P

EXPLICIT = False
MESH = pl.DeviceIdType.MESH
F32, BF16 = jnp.float32, jnp.bfloat16

ROWS = 256
D = 4608
F = 2304
KA, KB = D // 256, F // 256
T9 = 9
CH = D // 2
PARTS = ((0, 96), (96, 80), (176, 80))
SLOTS = 6
PIECE = 64
NP = ROWS // PIECE
LS = 12
ZERO = 63
LAST = 216


def _gelu_mul(g, u):
    t = jnp.tanh(0.7978845608028654 * (g + 0.044715 * (g * g * g)))
    return (g * (0.5 * (1.0 + t)) * u).astype(BF16)


def _kernel(
    x, wg, wu, wd, y, xall,
    xbuf, hid, ring, accbuf, d2s, d2r, ls, recv, emu,
    w_sem, x_sem, ag_send, ag_recv, ad_send, ad_recv, ds_sem, dr_sem, ls_sem, rs_recv,
    *accs,
):
    me = lax.axis_index("tp")
    core = lax.rem(me, 2)
    partner = me + 1 - 2 * core
    axes = [me + m * (1 - 2 * lax.rem(me // m, 2)) for m in (8, 4, 2)]
    nbr = [
        [jnp.where(core == 0, axes[(p + r) % 3], axes[(p + r + 1) % 3]) for r in range(3)]
        for p in range(3)
    ]
    acc = [
        [[accs[(q * 2 + h) * NP + r] for r in range(NP)] for h in range(2)] for q in range(2)
    ] if EXPLICIT else None

    def unit_start(p):
        s = lax.rem(p, SLOTS)
        v = lax.rem(p + 18, 27)
        early = p < 36
        gate_up = early | ((v >= 9) & (p < 198))
        i = jnp.where(early, lax.rem(p, 18), v - 9)
        j = jnp.where(v < 9, v, v - 9)

        @pl.when(gate_up)
        def _():
            cols = pl.ds(pl.multiple_of((i // 2) * 256, 256), 256)
            rows = pl.ds(pl.multiple_of(lax.rem(i, 2) * F, F), F)
            pltpu.make_async_copy(wg.at[rows, cols], ring.at[s, 0], w_sem.at[s, 0]).start()
            pltpu.make_async_copy(wu.at[rows, cols], ring.at[s, 1], w_sem.at[s, 1]).start()

        @pl.when(jnp.logical_not(gate_up) & (p < LAST))
        def _():
            for q in range(2):
                cols = pl.ds(pl.multiple_of(j * 512 + q * 256, 256), 256)
                pltpu.make_async_copy(wd.at[:, cols], ring.at[s, q], w_sem.at[s, q]).start()

    def unit_wait(p):
        s = lax.rem(p, SLOTS)
        for q in range(2):
            pltpu.make_async_copy(wd.at[:, pl.ds(0, 256)], ring.at[s, q], w_sem.at[s, q]).wait()

    def pop(q, h, r):
        if EXPLICIT:
            return pltpu.matmul_pop(acc[q][h][r])
        return emu[q, h, pl.ds(r * PIECE, PIECE), :]

    def half(h, lhs, depth, rhs, after, hooks):
        if not EXPLICIT:
            for k in sorted(hooks):
                hooks[k]()
            for q in range(2):
                tot = None
                for k in range(depth):
                    t = jnp.dot(lhs(h * ROWS, ROWS, k), rhs(q, k), preferred_element_type=F32)
                    tot = t if tot is None else tot + t
                emu[q, h] = tot
            return
        for k in range(depth):
            reg = (h * depth + k) % 2
            for r in range(NP):
                for q in range(2):
                    pltpu.matmul_acc_lhs(
                        acc[q][h][r],
                        lhs(h * ROWS + r * PIECE, PIECE, k),
                        load_staged_rhs=reg if r == 0 else None,
                    )
            for q in range(2):
                w = rhs(q, k + 1) if k + 1 < depth else after(q)
                pltpu.matmul_push_rhs(w, staging_register=1 - reg, mxu_index=q)
            if k in hooks:
                hooks[k]()

    def pop_hidden(h, hb, row0, j):
        cols = pl.ds(pl.multiple_of(j * 256, 256), 256)
        for r in range(NP):
            g, u = pop(0, h, r), pop(1, h, r)
            rows = pl.ds(pl.multiple_of(row0 + r * PIECE, PIECE), PIECE)
            hid[hb, rows, cols] = _gelu_mul(g, u)

    def pop_other(j):
        s = lax.rem(j, 3)
        for r in range(NP):
            for q in range(2):
                d2s[s, pl.ds(r * PIECE, PIECE), pl.ds(q * 256, 256)] = pop(q, 0, r).astype(BF16)

    def pop_own(j):
        for r in range(NP):
            for q in range(2):
                accbuf[j, pl.ds(r * PIECE, PIECE), pl.ds(q * 256, 256)] = pop(q, 1, r)

    def step_a(p, xs, first, second, mid=None, extra=None):
        s = [lax.rem(p + i, SLOTS) for i in range(3)]

        def lhs(row, n, k):
            return xbuf[xs, pl.ds(row, n), pl.ds(k * 256, 256)]

        def rhs(q, k):
            return ring[s[0] if k < 9 else s[1], q, pl.ds((k % 9) * 256, 256), :]

        half(0, lhs, KA, rhs, lambda q: rhs(q, 0), {1: first, **(extra or {})})
        if mid is not None:
            mid()
        half(1, lhs, KA, rhs, lambda q: ring[s[2], q, pl.ds(0, 256), :], {1: second})

    def step_b(p, hb, j, first, extra=None):
        s = [lax.rem(p + i, SLOTS) for i in range(2)]

        def lhs(row, n, k):
            return hid[hb, pl.ds(row, n), pl.ds(k * 256, 256)]

        def rhs(q, k):
            return ring[s[0], q, pl.ds(k * 256, 256), :]

        half(0, lhs, KB, rhs, lambda q: rhs(q, 0), {1: first, **(extra or {})})
        half(1, lhs, KB, rhs, lambda q: ring[s[1], q, pl.ds(0, 256), :], {1: lambda: pop_other(j)})

    def ag_start(src, dst, role, c):
        cols = pl.ds(c * CH, CH)
        for p, (o, n) in enumerate(PARTS):
            rows = pl.ds(o, n)
            pltpu.make_async_remote_copy(
                src_ref=x.at[rows, cols] if src == 0 else xall.at[src - 1, 0, rows, cols],
                dst_ref=xall.at[dst - 1, 0, rows, cols],
                send_sem=ag_send.at[dst - 1, c],
                recv_sem=ag_recv.at[dst - 1, c],
                device_id={"tp": nbr[p][role]},
                device_id_type=MESH,
            ).start()

    def ag_arrived(n, c):
        blk = xall.at[n - 1, 0, :, pl.ds(c * CH, CH)]
        pltpu.make_async_copy(blk, blk, ag_recv.at[n - 1, c]).wait()

    def pass_on(n, c):
        cols = pl.ds(c * CH, CH)
        dst = {0: xbuf.at[0, pl.ds(ROWS, ROWS), cols], 1: xbuf.at[1, pl.ds(0, ROWS), cols]}
        return pltpu.make_async_remote_copy(
            src_ref=x.at[:, cols] if n == 0 else xall.at[n - 1, 0, :, cols],
            dst_ref=dst[n] if n < 2 else xall.at[n - 1, 1, :, cols],
            send_sem=ad_send.at[n, c],
            recv_sem=ad_recv.at[n, c],
            device_id={"tp": partner},
            device_id_type=MESH,
        )

    def passed(n, c):
        blk = x.at[:, pl.ds(0, CH)]
        pltpu.make_async_copy(blk, blk, ad_recv.at[n, c]).wait()

    def x_load(n):
        xs = lax.rem(n, 2)
        return [
            pltpu.make_async_copy(
                xall.at[n - 1, 1 - h], xbuf.at[xs, pl.ds(h * ROWS, ROWS)], x_sem.at[h]
            )
            for h in range(2)
        ]

    def own_load(c):
        cols = pl.ds(c * CH, CH)
        return pltpu.make_async_copy(
            xall.at[0, 0, :, cols], xbuf.at[1, pl.ds(ROWS, ROWS), cols], x_sem.at[c]
        )

    def d2_start(n, j):
        s = lax.rem(j, 3)
        pltpu.make_async_remote_copy(
            src_ref=d2s.at[s],
            dst_ref=d2r.at[lax.rem(n, 2), j],
            send_sem=ds_sem.at[s],
            recv_sem=dr_sem.at[lax.rem(n, 2), j],
            device_id={"tp": partner},
            device_id_type=MESH,
        ).start()

    def d2_sent(j):
        s = lax.rem(j, 3)
        pltpu.make_async_copy(d2s.at[s], d2s.at[s], ds_sem.at[s]).wait()

    def d2_arrived(n, j):
        blk = d2r.at[lax.rem(n, 2), j]
        pltpu.make_async_copy(blk, blk, dr_sem.at[lax.rem(n, 2), j]).wait()

    def sum_start(n, j):
        s = lax.rem(9 * (n - 1) + j, LS)
        for p, (o, rows) in enumerate(PARTS):
            to = jnp.where(n <= 4, nbr[p][0], jnp.where(n <= 6, nbr[p][1], nbr[p][2]))
            pltpu.make_async_remote_copy(
                src_ref=ls.at[s, pl.ds(o, rows)],
                dst_ref=recv.at[9 * (n - 1) + j, pl.ds(o, rows)],
                send_sem=ls_sem.at[s],
                recv_sem=rs_recv.at[n - 1, j],
                device_id={"tp": to},
                device_id_type=MESH,
            ).start()

    def out_start(j):
        s = lax.rem(63 + j, LS)
        cols = pl.ds(pl.multiple_of(j * 512, 512), 512)
        pltpu.make_async_copy(ls.at[s], y.at[:, cols], ls_sem.at[s]).start()

    def sum_sent(g):
        s = lax.rem(g, LS)
        pltpu.make_async_copy(ls.at[s], ls.at[s], ls_sem.at[s]).wait()

    def rs_arrived(n, j):
        blk = recv.at[0]
        pltpu.make_async_copy(blk, blk, rs_recv.at[n - 1, j]).wait()

    def add(n, j, pages, lo, rows=32):
        s = lax.rem(9 * (n - 1) + j, LS)
        sl = pl.ds(lo, rows)
        v = accbuf[j, sl, :] + d2r[lax.rem(n, 2), j, sl, :].astype(F32)
        for g in pages:
            v = v + recv[g, sl, :].astype(F32)
        ls[s, sl, :] = v.astype(BF16)

    def adds(n, j, pages, ks):
        rows = ROWS // len(ks)
        return {
            k: functools.partial(add, n, j, pages, i * rows, rows) for i, k in enumerate(ks)
        }

    def late_pages(n, j):
        return (
            jnp.where(n == 7, 18, 0) + j,
            jnp.where(n == 7, 45, 36) + j,
            jnp.where(n == 7, ZERO, 54 + j),
        )

    def late_arrived(n, j):
        d2_arrived(n, j)

        @pl.when(n == 7)
        def _():
            rs_arrived(3, j)
            rs_arrived(6, j)

        @pl.when(n == 8)
        def _():
            rs_arrived(1, j)
            rs_arrived(5, j)
            rs_arrived(7, j)

    if EXPLICIT:
        for q in range(2):
            for h in range(2):
                for r in range(NP):
                    pop(q, h, r)
    else:
        emu[...] = jnp.zeros_like(emu)
    own = pltpu.make_async_copy(x, xbuf.at[0, pl.ds(0, ROWS)], x_sem.at[0])
    own.start()
    for p in range(SLOTS - 1):
        unit_start(jnp.int32(p))
    barrier = pltpu.get_barrier_semaphore()
    for d in (*axes, partner):
        pl.semaphore_signal(barrier, inc=1, device_id={"tp": d}, device_id_type=MESH)
    pl.semaphore_wait(barrier, 4)
    for c in range(2):
        pass_on(0, c).start()
    for c in range(2):
        ag_start(0, 1, 0, c)
    recv[ZERO] = jnp.zeros_like(recv[ZERO])
    own.wait()
    unit_wait(jnp.int32(0))
    if EXPLICIT:
        for q in range(2):
            pltpu.matmul_push_rhs(ring[0, q, pl.ds(0, 256), :], staging_register=0, mxu_index=q)

    def early(t, _):
        p = 2 * t
        n, j = t // 9, lax.rem(t, 9)
        before = lax.rem(t + 17, 18)
        unit_wait(p + 1)
        unit_wait(p + 2)

        @pl.when(t > 0)
        def _():
            unit_start(p + 4)

        unit_start(p + 5)

        @pl.when(t == 5)
        def _():
            ag_arrived(1, 0)
            pass_on(1, 0).start()
            own_load(0).start()
            ag_start(1, 2, 1, 0)

        @pl.when(t == 8)
        def _():
            ag_arrived(1, 1)
            pass_on(1, 1).start()
            own_load(1).start()
            ag_start(1, 2, 1, 1)
            ag_start(1, 3, 2, 0)
            ag_start(1, 3, 2, 1)

        @pl.when(t == 9)
        def _():
            for c in range(2):
                passed(1, c)
                own_load(c).wait()

        @pl.when(t == 12)
        def _():
            ag_arrived(2, 0)
            pass_on(2, 0).start()
            ag_start(2, 4, 2, 0)

        @pl.when(t == 16)
        def _():
            ag_arrived(2, 1)
            pass_on(2, 1).start()
            ag_start(2, 4, 2, 1)

        def mid():
            @pl.when(t == 0)
            def _():
                passed(0, 0)
                passed(0, 1)

        step_a(
            p,
            n,
            lambda: pop_hidden(
                1, before // 9, jnp.where(before < 9, 0, ROWS), lax.rem(before, 9)
            ),
            lambda: pop_hidden(0, n, jnp.where(n == 0, ROWS, 0), j),
            mid,
        )
        return 0

    lax.fori_loop(0, 18, early, 0)

    def block(n, _):
        base = 36 + 27 * (n - 1)
        unit_wait(base + 1)
        unit_start(base + 4)
        unit_start(base + 5)

        @pl.when(n > 1)
        def _():
            sum_start(n - 1, 8)
            d2_sent(0)

        @pl.when(n < 7)
        def _():
            passed(n + 1, 0)
            passed(n + 1, 1)
            for copy in x_load(n + 1):
                copy.start()

        @pl.when(n == 1)
        def _():
            ag_start(0, 5, 1, 0)
            ag_start(0, 5, 1, 1)

        @pl.when(n == 2)
        def _():
            for c in range(2):
                ag_arrived(4, c)
                pass_on(4, c).start()

        @pl.when(n == 3)
        def _():
            ag_start(0, 7, 2, 0)
            ag_start(0, 7, 2, 1)

        @pl.when(n == 4)
        def _():
            for c in range(2):
                ag_arrived(6, c)
                pass_on(6, c).start()

        @pl.when(n == 5)
        def _():
            for c in range(2):
                ag_arrived(7, c)
                pass_on(7, c).start()

        step_b(base, 1, 0, lambda: pop_hidden(1, 1, ROWS, 8))

        def down(j, _):
            p = base + j
            unit_wait(p + 1)
            unit_start(p + 5)
            d2_start(n, j - 1)

            @pl.when((n > 1) | (j >= 3))
            def _():
                d2_sent(j)

            step_b(p, 1, j, lambda: pop_own(j - 1))
            return 0

        lax.fori_loop(1, jnp.where(n == 7, 3, 9), down, 0)

        @pl.when(n < 7)
        def _():
            mark = base + 9

            def ready(j):
                @pl.when(9 * (n - 1) + j >= LS)
                def _():
                    sum_sent(9 * (n - 1) + j)

                d2_arrived(n, j)

                @pl.when(n == 5)
                def _():
                    rs_arrived(2, j)

                @pl.when(n == 6)
                def _():
                    rs_arrived(4, j)

            def page(j):
                return (jnp.where(n == 5, 9 + j, jnp.where(n == 6, 27 + j, ZERO)),)

            xs = lax.rem(n + 1, 2)
            ks = (3, 5, 7, 9, 11, 13, 15, 16)
            unit_wait(mark + 1)
            unit_wait(mark + 2)
            unit_start(mark + 5)
            d2_start(n, 8)
            for copy in x_load(n + 1):
                copy.wait()

            @pl.when(n == 1)
            def _():
                for c in range(2):
                    ag_arrived(3, c)
                    pass_on(3, c).start()

            @pl.when(n == 2)
            def _():
                for c in range(2):
                    ag_arrived(5, c)
                    pass_on(5, c).start()
                    ag_start(5, 6, 2, c)

            ready(0)
            step_a(
                mark, xs, lambda: pop_own(8), lambda: pop_hidden(0, 1, 0, 0),
                extra=adds(n, 0, page(0), ks),
            )

            def gate_up(j, _):
                p = mark + 2 * j
                unit_wait(p + 1)
                unit_wait(p + 2)
                unit_start(p + 4)
                unit_start(p + 5)
                sum_start(n, j - 1)
                ready(j)
                step_a(
                    p, xs, lambda: pop_hidden(1, 1, ROWS, j - 1), lambda: pop_hidden(0, 1, 0, j),
                    extra=adds(n, j, page(j), ks),
                )
                return 0

            lax.fori_loop(1, 9, gate_up, 0)

        return 0

    lax.fori_loop(1, 8, block, 0)

    def out_or_on(i):
        @pl.when(i < 9)
        def _():
            sum_start(7, i)

        @pl.when(i >= 9)
        def _():
            out_start(i - 9)

    def late(t, _):
        p = 198 + t

        @pl.when(t < 17)
        def _():
            unit_wait(p + 1)

        unit_start(p + 5)
        d2_start(7 + (t - 1) // 9, lax.rem(t - 1, 9))
        d2_sent(lax.rem(t, 9))

        @pl.when(t > 3)
        def _():
            out_or_on(t - 4)

        i = t - 3
        n, j = 7 + i // 9, lax.rem(i, 9)
        sum_sent(54 + i)
        late_arrived(n, j)
        step_b(
            p, jnp.where(t < 9, 1, 0), lax.rem(t, 9), lambda: pop_own(lax.rem(t - 1, 9)),
            extra=adds(n, j, late_pages(n, j), (2, 3, 4, 5, 6, 7, 8)[:4]),
        )
        return 0

    lax.fori_loop(3, 18, late, 0)

    d2_start(jnp.int32(8), jnp.int32(8))
    out_or_on(jnp.int32(14))
    if EXPLICIT:
        for q in range(2):
            pltpu.matmul_acc_lhs(acc[q][0][0], xbuf[0, pl.ds(0, PIECE), pl.ds(0, 256)], load_staged_rhs=0)
            pop(q, 0, 0)
    pop_own(8)
    for j in (6, 7, 8):
        sum_sent(jnp.int32(63 + j))
        late_arrived(jnp.int32(8), jnp.int32(j))
        for lo in range(0, ROWS, 32):
            add(jnp.int32(8), jnp.int32(j), late_pages(jnp.int32(8), j), lo)
        out_start(jnp.int32(j))

    for g in range(60, 72):
        sum_sent(jnp.int32(g))
    for j in (6, 7, 8):
        d2_sent(jnp.int32(j))
    blk = x.at[:, pl.ds(0, CH)]
    for c in range(2):
        for n in range(8):
            pltpu.make_async_copy(blk, blk, ad_send.at[n, c]).wait()
            if n:
                pltpu.make_async_copy(blk, blk, ag_send.at[n - 1, c]).wait()


def _call(x, wg, wu, wd):
    dma = pltpu.SemaphoreType.DMA
    emu_shape = (2, 2, ROWS, 256) if not EXPLICIT else (1, 1, 8, 128)

    def body(*refs):
        if not EXPLICIT:
            _kernel(*refs)
            return
        specs = [pltpu.ACC(q)((PIECE, 256), F32) for q in range(2) for _ in range(2 * NP)]
        pl.run_scoped(lambda *accs: _kernel(*refs, *accs), *specs)

    return pl.pallas_call(
        body,
        out_shape=(
            jax.ShapeDtypeStruct((ROWS, D), BF16),
            jax.ShapeDtypeStruct((7, 2, ROWS, D), BF16),
        ),
        in_specs=[pl.BlockSpec(memory_space=pltpu.HBM)] * 4,
        out_specs=[pl.BlockSpec(memory_space=pltpu.HBM)] * 2,
        scratch_shapes=[
            pltpu.VMEM((2, 2 * ROWS, D), BF16),
            pltpu.VMEM((2, 2 * ROWS, F), BF16),
            pltpu.VMEM((SLOTS, 2, F, 256), BF16),
            pltpu.VMEM((9, ROWS, 512), F32),
            pltpu.VMEM((3, ROWS, 512), BF16),
            pltpu.VMEM((2, 9, ROWS, 512), BF16),
            pltpu.VMEM((LS, ROWS, 512), BF16),
            pltpu.VMEM((64, ROWS, 512), BF16),
            pltpu.VMEM(emu_shape, F32),
            dma((SLOTS, 2)),
            dma((2,)),
            dma((7, 2)),
            dma((7, 2)),
            dma((8, 2)),
            dma((8, 2)),
            dma((3,)),
            dma((2, 9)),
            dma((LS,)),
            dma((7, 9)),
        ],
        compiler_params=pltpu.CompilerParams(
            collective_id=0, has_side_effects=True, vmem_limit_bytes=67_000_000
        ),
        name="mlp",
    )(x, wg, wu, wd)[0]


def solution(mesh):
    return jax.shard_map(
        _call,
        mesh=mesh,
        in_specs=(P(("dp", "tp"), None), P(None, "tp"), P(None, "tp"), P("tp", None)),
        out_specs=P(("dp", "tp"), None),
        check_vma=False,
    )
```

time: 667 us -> 324 us (0.49)
  waiting for transfers between devices: 353 us -> 0 us
  Pallas kernels: 0 us -> 320 us
  matrix products: 300 us -> 0 us
  between operations: 13.4 us -> 0.01 us
    pallas_call x0 -> x1, Pallas kernels: none -> 320 us  [_call(): pl.pallas_call(body, out_shape=(jax.ShapeDtypeStruct((ROWS, D), BF16), ja...]
    dot_general x3 -> x0, matrix products: 300 us -> none  [the longest x1 104 us: step(): up = jnp.dot(rows, w_up, preferred_element_type=jnp.float32)]
    reduce_scatter x1 -> x0, waiting for transfers between devices: 202 us -> none  [step(): return lax.psum_scatter(term, 'tp', scatter_dimension=0, tiled=True)]
    all_gather x1 -> x0, waiting for transfers between devices: 150 us -> none  [step(): rows = lax.all_gather(x, 'tp', axis=0, tiled=True)]
  transfers between devices with their start and end apart: 2 -> 0, of which waited for: 2 -> 0; matrix products, arithmetic and copies ran while one was open for 0% -> 0% of each run, Pallas kernels for 0% -> 0%
where the time goes in v1:
time: 324 us
  Pallas kernels  320 us (99%)
    pallas_call x1, Pallas kernels, _call(): pl.pallas_call(body, out_shape=(jax.ShapeDtypeStruct((ROWS, D), BF16), ja...  320 us

profile of v1, /device:TPU:0, one launch (start us, length us, event | category | flops | bytes accessed | tf_op | source)
XLA Modules:
  0.0 323.7 jit_solution(12687577458386158240)
XLA Ops:
  0.0 320.5 %mlp.1 = (bf16[256,4608]{1,0:T(8,128)(2,1)}, bf16[7,2,256,4608]{3,2,1,0:T(8,128)(2,1)}) custom-call(bf16[256,4608]{1,0:T(8,128)(2,1)} %refs_0_.1, bf16[4608,2304]{1,0:T(8,128)(2,1)} %refs_1_.1, bf16[4608,2304]{1,0:T(8,128)(2,1)} %refs_2_.1, bf16[2304,4608]{1,0:T(8,128)(2,1)} %refs_3_.1), custom_call_target="tpu_custom_call" | custom-call | tf_op jit(solution)/shard_map/mlp/pallas_call | solution.py:579
  320.5 3.2 copy.6

commit v2 on v0

v2 whole, which is shorter than its diff:
```python
import functools

import jax
import jax.numpy as jnp
from jax import lax
from jax.experimental import pallas as pl
from jax.experimental.pallas import tpu as pltpu
from jax.sharding import PartitionSpec as P

MESH = pl.DeviceIdType.MESH
F32, BF16 = jnp.float32, jnp.bfloat16

ROWS = 256
D = 4608
F = 2304
T = 256
KA, KB = D // T, F // T
W = 3 * T
V = 6 * T
CH = D // 2
PARTS = ((0, 96), (96, 80), (176, 80))
RING = 4
EARLY = 12
FINAL = 66
CHUNKS = 72
LS = 4
A, B, C = range(3)


def _gelu_mul(g, u):
    t = jnp.tanh(0.7978845608028654 * (g + 0.044715 * (g * g * g)))
    return (g * (0.5 * (1.0 + t)) * u).astype(BF16)


def _kernel(
    x, wg, wu, wd, y, xall, rbuf,
    xbuf, hid, ring, accbuf, d2s, d2r, ls, rsum, rlate,
    w_sem, f_sem, x_sem, r_sem, ag_send, ag_recv, ad_send, ad_recv, ds_sem, dr_sem, ls_sem, rs_recv,
):
    me = lax.axis_index("tp")
    core = lax.rem(me, 2)
    partner = me + 1 - 2 * core
    axes = [me + m * (1 - 2 * lax.rem(me // m, 2)) for m in (8, 4, 2)]
    nbr = [
        [jnp.where(core == 0, axes[(p + r) % 3], axes[(p + r + 1) % 3]) for r in range(3)]
        for p in range(3)
    ]

    def local(src, dst, sem):
        return pltpu.make_async_copy(src, dst, sem)

    def await_bytes(ref, sem):
        pltpu.make_async_copy(ref, ref, sem).wait()

    def remote(src, dst, send, recv, to):
        return pltpu.make_async_remote_copy(
            src_ref=src, dst_ref=dst, send_sem=send, recv_sem=recv,
            device_id={"tp": to}, device_id_type=MESH,
        )

    def chunk_start(p):
        s = lax.rem(p, RING)
        v = lax.rem(p + 6, 9)
        early = p < EARLY
        gate_up = early | ((v > 2) & (p < FINAL))
        i = jnp.where(early, lax.rem(p, 6), v - 3)
        j = jnp.where(v > 2, v - 3, v)

        def start(w):
            cols = pl.ds(pl.multiple_of((i // 2) * W, T), W)
            for d in range(2):
                local(
                    w.at[pl.ds(d * F, F), cols], ring.at[s, :, pl.ds(d * W, W)], w_sem.at[s]
                ).start()

        pl.when(gate_up & (lax.rem(i, 2) == 0))(lambda: start(wg))
        pl.when(gate_up & (lax.rem(i, 2) == 1))(lambda: start(wu))

        @pl.when(jnp.logical_not(gate_up) & (p < CHUNKS))
        def _():
            local(wd.at[:, pl.ds(pl.multiple_of(j * V, T), V)], ring.at[s], w_sem.at[s]).start()

    def chunk_wait(p):
        s = lax.rem(p, RING)
        await_bytes(ring.at[s], w_sem.at[s])

    def product(lhs, rhs, depth):
        total = None
        for k in range(depth):
            t = jnp.dot(lhs(k), rhs(k), preferred_element_type=F32)
            total = t if total is None else total + t
        return total

    def tile_a(p, xs, row, i, hb, hrow, j):
        sl = [lax.rem(p + q, RING) for q in range(2)]

        def lhs(k):
            return xbuf[xs, pl.ds(row, ROWS), pl.ds(k * T, T)]

        def rhs(q):
            def tile(k):
                at = pl.multiple_of((k // KB) * W + i * T, T) if not isinstance(i, int) else (k // KB) * W + i * T
                return ring[sl[q], pl.ds((k % KB) * T, T), pl.ds(at, T)]

            return tile

        g, u = product(lhs, rhs(0), KA), product(lhs, rhs(1), KA)
        hid[hb, pl.ds(hrow, ROWS), pl.ds(pl.multiple_of(j * T, T), T)] = _gelu_mul(g, u)

    def step_a(p, xs, hb, flip, e, extra=None):
        for i in range(3):
            for h in range(2):
                row = h * ROWS
                hrow = pl.multiple_of(jnp.where(flip, ROWS - row, row), ROWS)
                tile_a(p, xs, row, i, hb, hrow, 3 * e + i)
                if extra is not None:
                    extra(2 * i + h)

    def step_b(p, hb, j, slot, extra=None):
        s = lax.rem(p, RING)
        for i in range(6):
            for h in range(2):

                def lhs(k, h=h):
                    return hid[hb, pl.ds(h * ROWS, ROWS), pl.ds(k * T, T)]

                def rhs(k, i=i):
                    return ring[s, pl.ds(k * T, T), pl.ds(i * T, T)]

                v = product(lhs, rhs, KB)
                if h == 0:
                    d2s[slot, :, pl.ds(i * T, T)] = v.astype(BF16)
                else:
                    accbuf[:, pl.ds(pl.multiple_of(j * V + i * T, T), T)] = v
            if extra is not None:
                extra(i)

    def ag_start(src, dst, role, c):
        cols = pl.ds(c * CH, CH)
        for p, (o, n) in enumerate(PARTS):
            rows = pl.ds(o, n)
            remote(
                x.at[rows, cols] if src == 0 else xall.at[src - 1, 0, rows, cols],
                xall.at[dst - 1, 0, rows, cols],
                ag_send.at[dst - 1, c],
                ag_recv.at[dst - 1, c],
                nbr[p][role],
            ).start()

    def ag_arrived(n, c):
        await_bytes(xall.at[n - 1, 0, :, pl.ds(c * CH, CH)], ag_recv.at[n - 1, c])

    def pass_on(n, c):
        cols = pl.ds(c * CH, CH)
        if n < 2:
            dst = xbuf.at[n, pl.ds((1 - n) * ROWS, ROWS), cols]
        else:
            dst = xall.at[n - 1, 1, :, cols]
        src = x.at[:, cols] if n == 0 else xall.at[n - 1, 0, :, cols]
        remote(src, dst, ad_send.at[n, c], ad_recv.at[n, c], partner).start()

    def passed(n, c):
        await_bytes(x.at[:, pl.ds(0, CH)], ad_recv.at[n, c])

    def relay(n):
        for c in range(2):
            ag_arrived(n, c)
            pass_on(n, c)

    def x_load(n):
        xs = lax.rem(n, 2)
        return [
            local(xall.at[n - 1, 1 - h], xbuf.at[xs, pl.ds(h * ROWS, ROWS)], x_sem.at[h])
            for h in range(2)
        ]

    def own_load(c):
        cols = pl.ds(c * CH, CH)
        return local(xall.at[0, 0, :, cols], xbuf.at[1, pl.ds(ROWS, ROWS), cols], x_sem.at[c])

    def cols_of(j):
        return pl.ds(pl.multiple_of(j * V, T), V)

    def d2_start(n, j, slot):
        remote(
            d2s.at[slot],
            d2r.at[lax.rem(n, 2), :, cols_of(j)],
            ds_sem.at[slot],
            dr_sem.at[lax.rem(n, 2), j],
            partner,
        ).start()

    def d2_sent(slot):
        await_bytes(d2s.at[slot], ds_sem.at[slot])

    def d2_arrived(n, j):
        await_bytes(d2s.at[0], dr_sem.at[lax.rem(n, 2), j])

    def sum_start(n, j, role, dst):
        s = lax.rem(3 * (n - 1) + j, LS)
        for p, (o, rows) in enumerate(PARTS):
            to = nbr[p][role] if isinstance(role, int) else jnp.where(role, nbr[p][A], nbr[p][B])
            remote(
                ls.at[s, pl.ds(o, rows)],
                dst.at[pl.ds(o, rows), cols_of(j)],
                ls_sem.at[s],
                rs_recv.at[n - 1, j],
                to,
            ).start()

    def sum_on(n, j):
        pl.when(n < 6)(
            lambda: sum_start(n, j, n < 5, rbuf.at[jnp.where(n < 6, n - 1, 0)])
        )
        pl.when(n == 6)(lambda: sum_start(n, j, B, rlate.at[0]))

    def out_start(j):
        s = lax.rem(21 + j, LS)
        local(ls.at[s], y.at[:, cols_of(j)], ls_sem.at[s]).start()

    def sum_sent(g):
        s = lax.rem(g, LS)
        await_bytes(ls.at[s], ls_sem.at[s])

    def rs_arrived(n, j):
        await_bytes(d2s.at[0], rs_recv.at[n - 1, j])

    def add(n, j, terms, i, rows):
        s = lax.rem(3 * (n - 1) + j, LS)
        sl, cols = pl.ds(i * rows, rows), cols_of(j)
        v = accbuf[sl, cols] + d2r[lax.rem(n, 2), sl, cols].astype(F32)
        for ref, r0 in terms:
            v = v + ref[pl.ds(r0 + i * rows, rows), cols].astype(F32)
        ls[s, sl, :] = v.astype(BF16)

    terms_c = ((xbuf.at[0], 0), (rlate.at[0], 0))
    terms_0 = ((xbuf.at[0], ROWS), (xbuf.at[1], 0), (rlate.at[1], 0))
    late_loads = ((2, xbuf.at[0, pl.ds(0, ROWS)]), (0, xbuf.at[0, pl.ds(ROWS, ROWS)]), (4, xbuf.at[1, pl.ds(0, ROWS)]))

    own = local(x, xbuf.at[0, pl.ds(0, ROWS)], x_sem.at[0])
    own.start()
    for i in range(3):
        for q, w in enumerate((wg, wu)):
            for d in range(2):
                local(
                    w.at[pl.ds(d * F, F), pl.ds(i * T, T)],
                    ring.at[q, :, pl.ds(d * W + i * T, T)],
                    f_sem.at[i],
                ).start()
    for p in range(2, RING):
        chunk_start(jnp.int32(p))
    barrier = pltpu.get_barrier_semaphore()
    for d in (*axes, partner):
        pl.semaphore_signal(barrier, inc=1, device_id={"tp": d}, device_id_type=MESH)
    pl.semaphore_wait(barrier, 4)
    for c in range(2):
        pass_on(0, c)
    for c in range(2):
        ag_start(0, 1, A, c)
    rsum[...] = jnp.zeros_like(rsum)
    own.wait()

    def pieces(e):
        first = e == 0

        @pl.when(jnp.logical_not(first))
        def _():
            for q in range(2):
                chunk_wait(2 * e + q)
                chunk_start(2 * e + q + 2)

        def piece(m, _):
            h, i = m // 3, lax.rem(m, 3)

            @pl.when(first & (h == 0))
            def _():
                await_bytes(ring.at[0, :, pl.ds(0, 4 * T)], f_sem.at[i])

            @pl.when(first & (m == 3))
            def _():
                passed(0, 0)
                passed(0, 1)

            for c in range(2):
                @pl.when(jnp.logical_not(first) & (m == 3 * c))
                def _():
                    ag_arrived(1, c)
                    pass_on(1, c)
                    own_load(c).start()
                    ag_start(1, 2, B, c)
                    if c:
                        ag_start(1, 3, C, 0)
                        ag_start(1, 3, C, 1)

            row = pl.multiple_of(h * ROWS, ROWS)
            hrow = pl.multiple_of(ROWS - h * ROWS, ROWS)
            tile_a(2 * e, 0, row, i, 0, hrow, 3 * e + i)
            return 0

        lax.fori_loop(0, 6, piece, 0)

    def early(e, _):
        p = 2 * e
        chunk_wait(p)
        chunk_wait(p + 1)
        chunk_start(p + 2)
        chunk_start(p + 3)

        @pl.when(e == 3)
        def _():
            for c in range(2):
                passed(1, c)
                own_load(c).wait()

        for c in range(2):
            @pl.when(e == 4 + c)
            def _():
                ag_arrived(2, c)
                pass_on(2, c)
                ag_start(2, 4, C, c)

        n = e // 3
        step_a(p, n, n, n == 0, lax.rem(e, 3))
        return 0

    def opening(g, _):
        pieces(2 * g)
        lax.fori_loop(2 * g + 1, 4 * g + 2, early, 0)
        return 0

    lax.fori_loop(0, 2, opening, 0)

    def block(n, _):
        base = EARLY + 9 * (n - 1)

        def down(j, _):
            p = base + j
            slot = lax.rem(n + j, 2)
            chunk_wait(p)
            pl.when(j == 0)(lambda: chunk_start(p + 2))
            chunk_start(p + 3)

            @pl.when(j > 0)
            def _():
                d2_start(n, j - 1, 1 - slot)

            @pl.when((n > 1) | (j > 1))
            def _():
                d2_sent(slot)

            @pl.when(j == 0)
            def _():
                @pl.when(n > 1)
                def _():
                    sum_on(n - 1, 2)

                @pl.when(n < 7)
                def _():
                    passed(n + 1, 0)
                    passed(n + 1, 1)
                    for copy in x_load(n + 1):
                        copy.start()

                @pl.when(n == 1)
                def _():
                    ag_start(0, 5, B, 0)
                    ag_start(0, 5, B, 1)

                @pl.when(n == 3)
                def _():
                    ag_start(0, 7, C, 0)
                    ag_start(0, 7, C, 1)

                for m, blk in ((2, 4), (4, 6), (5, 7)):
                    pl.when(n == m)(functools.partial(relay, blk))

                for m, src in ((5, 2), (6, 4)):
                    @pl.when(n == m)
                    def _():
                        for i in range(3):
                            rs_arrived(src, i)
                        local(rbuf.at[src - 1], rsum, r_sem.at[0]).start()

                @pl.when(n == 7)
                def _():
                    for i, (src, dst) in enumerate(late_loads):
                        for k in range(3):
                            rs_arrived(src + 1, k)
                        local(rbuf.at[src], dst, r_sem.at[i]).start()

            step_b(p, 1, j, slot)
            return 0

        lax.fori_loop(0, jnp.where(n == 7, 1, 3), down, 0)

        def gate_up(j, _):
            p = base + 3 + 2 * j
            chunk_wait(p)
            chunk_wait(p + 1)
            pl.when(j > 0)(lambda: chunk_start(p + 2))
            chunk_start(p + 3)

            @pl.when(j > 0)
            def _():
                sum_on(n, j - 1)

            @pl.when(j == 0)
            def _():
                d2_start(n, 2, lax.rem(n, 2))
                for copy in x_load(n + 1):
                    copy.wait()

                @pl.when(n > 4)
                def _():
                    local(rbuf.at[0], rsum, r_sem.at[0]).wait()

                pl.when(n == 1)(lambda: relay(3))

                @pl.when(n == 2)
                def _():
                    relay(5)
                    for c in range(2):
                        ag_start(5, 6, C, c)

            @pl.when(3 * (n - 1) + j >= LS)
            def _():
                sum_sent(3 * (n - 1) + j)

            d2_arrived(n, j)

            def extra(i):
                if i < 4:
                    add(n, j, ((rsum, 0),), i, ROWS // 4)

            step_a(p, lax.rem(n + 1, 2), 1, False, j, extra)
            return 0

        lax.fori_loop(0, jnp.where(n == 7, 0, 3), gate_up, 0)
        return 0

    lax.fori_loop(1, 8, block, 0)

    def late(n):
        def step(t, _):
            p = FINAL + t
            slot = lax.rem(t + 1, 2)
            chunk_wait(p)
            chunk_start(p + 3)
            d2_start(7 + (t - 1) // 3, lax.rem(t - 1, 3), 1 - slot)
            d2_sent(slot)
            j = lax.rem(t - 1, 3)
            if n == 7:
                pl.when(t > 1)(lambda: sum_start(7, t - 2, C, rlate.at[1]))

                @pl.when(t == 1)
                def _():
                    for i, (src, dst) in enumerate(late_loads):
                        local(rbuf.at[src], dst, r_sem.at[i]).wait()

                rs_arrived(6, j)
            else:
                pl.when(t == 4)(lambda: sum_start(7, 2, C, rlate.at[1]))
                pl.when(t > 4)(lambda: out_start(t - 5))
                rs_arrived(7, j)
            sum_sent(3 * (n - 1) + j)
            d2_arrived(n, j)

            def extra(i):
                if i < 4:
                    add(n, j, terms_c if n == 7 else terms_0, i, ROWS // 4)

            step_b(p, jnp.where(t < 3, 1, 0), lax.rem(t, 3), slot, extra)
            return 0

        return step

    lax.fori_loop(1, 4, late(7), 0)
    lax.fori_loop(4, 6, late(8), 0)

    last = jnp.int32(2)
    d2_start(jnp.int32(8), last, 0)
    out_start(1)
    sum_sent(23)
    d2_arrived(jnp.int32(8), last)
    rs_arrived(7, 2)
    for i in range(8):
        add(jnp.int32(8), 2, terms_0, i, ROWS // 8)
    out_start(2)

    for s in range(LS):
        sum_sent(s)
    d2_sent(0)
    d2_sent(1)
    for c in range(2):
        for n in range(8):
            await_bytes(x.at[:, pl.ds(0, CH)], ad_send.at[n, c])
            if n:
                await_bytes(x.at[:, pl.ds(0, CH)], ag_send.at[n - 1, c])


def _call(x, wg, wu, wd):
    dma = pltpu.SemaphoreType.DMA
    rows = (ROWS, D)
    return pl.pallas_call(
        _kernel,
        out_shape=tuple(
            jax.ShapeDtypeStruct(shape, BF16) for shape in (rows, (7, 2, *rows), (5, *rows))
        ),
        in_specs=[pl.BlockSpec(memory_space=pltpu.HBM)] * 4,
        out_specs=[pl.BlockSpec(memory_space=pltpu.HBM)] * 3,
        scratch_shapes=[
            pltpu.VMEM((2, 2 * ROWS, D), BF16),
            pltpu.VMEM((2, 2 * ROWS, F), BF16),
            pltpu.VMEM((RING, F, V), BF16),
            pltpu.VMEM(rows, F32),
            pltpu.VMEM((2, ROWS, V), BF16),
            pltpu.VMEM((2, *rows), BF16),
            pltpu.VMEM((LS, ROWS, V), BF16),
            pltpu.VMEM(rows, BF16),
            pltpu.VMEM((2, *rows), BF16),
            *(dma(s) for s in ((RING,), (3,), (2,), (3,), (7, 2), (7, 2), (8, 2), (8, 2), (2,), (2, 3), (LS,), (7, 3))),
        ],
        compiler_params=pltpu.CompilerParams(
            collective_id=0, has_side_effects=True, vmem_limit_bytes=67_000_000
        ),
        name="mlp",
    )(x, wg, wu, wd)[0]


def solution(mesh):
    return jax.shard_map(
        _call,
        mesh=mesh,
        in_specs=(P(("dp", "tp"), None), P(None, "tp"), P(None, "tp"), P("tp", None)),
        out_specs=P(("dp", "tp"), None),
        check_vma=False,
    )
```

time: 667 us -> 317 us (0.48)
  waiting for transfers between devices: 353 us -> 0 us
  Pallas kernels: 0 us -> 314 us
  matrix products: 300 us -> 0 us
  between operations: 13.4 us -> 0.01 us
    pallas_call x0 -> x1, Pallas kernels: none -> 314 us  [_call(): pl.pallas_call(_kernel, out_shape=tuple((jax.ShapeDtypeStruct(shape, BF16...]
    dot_general x3 -> x0, matrix products: 300 us -> none  [the longest x1 104 us: step(): up = jnp.dot(rows, w_up, preferred_element_type=jnp.float32)]
    reduce_scatter x1 -> x0, waiting for transfers between devices: 202 us -> none  [step(): return lax.psum_scatter(term, 'tp', scatter_dimension=0, tiled=True)]
    all_gather x1 -> x0, waiting for transfers between devices: 150 us -> none  [step(): rows = lax.all_gather(x, 'tp', axis=0, tiled=True)]
  transfers between devices with their start and end apart: 2 -> 0, of which waited for: 2 -> 0; matrix products, arithmetic and copies ran while one was open for 0% -> 0% of each run, Pallas kernels for 0% -> 0%
where the time goes in v2:
time: 317 us
  Pallas kernels  314 us (99%)
  local copies, waits for them, and re-layouts  3.22 us (1%)
    pallas_call x1, Pallas kernels, _call(): pl.pallas_call(_kernel, out_shape=tuple((jax.ShapeDtypeStruct(shape, BF16...  314 us

profile of v2, /device:TPU:0, one launch (start us, length us, event | category | flops | bytes accessed | tf_op | source)
XLA Modules:
  0.0 317.4 jit_solution(11615348314005206865)
XLA Ops:
  0.0 314.1 %mlp.1 = (bf16[256,4608]{1,0:T(8,128)(2,1)}, bf16[7,2,256,4608]{3,2,1,0:T(8,128)(2,1)}, bf16[5,256,4608]{2,1,0:T(8,128)(2,1)}) custom-call(bf16[256,4608]{1,0:T(8,128)(2,1)} %x.1, bf16[4608,2304]{1,0:T(8,128)(2,1)} %wg.1, bf16[4608,2304]{1,0:T(8,128)(2,1)} %wu.1, bf16[2304,4608]{1,0:T(8,128)(2,1)} %wd.1), custom_call_target="tpu_custom_call" | custom-call | tf_op jit(solution)/shard_map/mlp/pallas_call | solution.py:504
  314.1 3.2 %copy.6 = bf16[256,4608]{1,0:T(8,128)(2,1)} copy(bf16[256,4608]{1,0:T(8,128)(2,1)} %get-tuple-element.6) | data formatting | bytes 4718592

commit v3 on v2

v3 whole, which is shorter than its diff:
```python
import functools

import jax
import jax.numpy as jnp
from jax import lax
from jax.experimental import pallas as pl
from jax.experimental.pallas import tpu as pltpu
from jax.sharding import PartitionSpec as P

MESH = pl.DeviceIdType.MESH
F32, BF16 = jnp.float32, jnp.bfloat16

ROWS = 256
D = 4608
F = 2304
T = 256
KA, KB = D // T, F // T
W = 3 * T
V = 6 * T
CH = D // 2
PARTS = ((0, 96), (96, 80), (176, 80))
RING = 4
EARLY = 12
FINAL = 66
LS = 4
A, B, C = range(3)


def _gelu_mul(g, u):
    t = jnp.tanh(0.7978845608028654 * (g + 0.044715 * (g * g * g)))
    return (g * (0.5 * (1.0 + t)) * u).astype(BF16)


def _when(cond):
    def run(f):
        def trip(_, carry):
            f()
            return carry

        lax.fori_loop(0, jnp.where(cond, 1, 0), trip, 0)

    return run


def _kernel(
    x, wg, wu, wd, y, xall, rbuf,
    xbuf, hub, ring, accbuf, d2s, ls, rsum, rlate,
    w_sem, f_sem, x_sem, r_sem, ag_send, ag_recv, ad_send, ad_recv, ds_sem, dr_sem, ls_sem, rs_recv,
):
    me = lax.axis_index("tp")
    core = lax.rem(me, 2)
    partner = me + 1 - 2 * core
    axes = [me + m * (1 - 2 * lax.rem(me // m, 2)) for m in (8, 4, 2)]
    nbr = [
        [jnp.where(core == 0, axes[(p + r) % 3], axes[(p + r + 1) % 3]) for r in range(3)]
        for p in range(3)
    ]

    def local(src, dst, sem):
        return pltpu.make_async_copy(src, dst, sem)

    def await_bytes(ref, sem):
        pltpu.make_async_copy(ref, ref, sem).wait()

    def remote(src, dst, send, recv, to):
        return pltpu.make_async_remote_copy(
            src_ref=src, dst_ref=dst, send_sem=send, recv_sem=recv,
            device_id={"tp": to}, device_id_type=MESH,
        )

    def load_one(w, i, p):
        s = lax.rem(p, RING)
        cols = pl.ds(pl.multiple_of(i * W, T), W)
        for d in range(2):
            local(
                w.at[pl.ds(d * F, F), cols], ring.at[s, :, pl.ds(d * W, W)], w_sem.at[s]
            ).start()

    def load_pair(i, p):
        load_one(wg, i, p)
        load_one(wu, i, p + 1)

    def load_down(j, p):
        s = lax.rem(p, RING)
        local(wd.at[:, pl.ds(j * V, V)], ring.at[s], w_sem.at[s]).start()

    def chunk_wait(p):
        s = lax.rem(p, RING)
        await_bytes(ring.at[s], w_sem.at[s])

    def product(lhs, rhs, depth):
        total = None
        for k in range(depth):
            t = jnp.dot(lhs(k), rhs(k), preferred_element_type=F32)
            total = t if total is None else total + t
        return total

    def tile_a(p, xs, row, i, hb, half, j):
        sl = [lax.rem(p + q, RING) for q in range(2)]

        def lhs(k):
            return xbuf[xs, pl.ds(row, ROWS), pl.ds(k * T, T)]

        def rhs(q):
            def tile(k):
                at = pl.multiple_of((k // KB) * W + i * T, T) if not isinstance(i, int) else (k // KB) * W + i * T
                return ring[sl[q], pl.ds((k % KB) * T, T), pl.ds(at, T)]

            return tile

        g, u = product(lhs, rhs(0), KA), product(lhs, rhs(1), KA)
        hub[hb, :, pl.ds(pl.multiple_of(half * F + j * T, T), T)] = _gelu_mul(g, u)

    def step_a(p, xs, hb, flip, e, extra=None):
        for i in range(3):
            for h in range(2):
                tile_a(p, xs, h * ROWS, i, hb, jnp.where(flip, 1 - h, h), 3 * e + i)
                if extra is not None:
                    extra(2 * i + h)

    def step_b(p, j, slot):
        s = lax.rem(p, RING)
        for i in range(6):
            d2s[slot, :, pl.ds(i * T, T)] = rows_b(1, 0, i, s).astype(BF16)
            accbuf[:, pl.ds(pl.multiple_of(j * V + i * T, T), T)] = rows_b(1, 1, i, s)

    def rows_b(hb, h, i, s):
        def lhs(k):
            return hub[hb, :, pl.ds(h * F + k * T, T)]

        def rhs(k):
            return ring[s, pl.ds(k * T, T), pl.ds(i * T, T)]

        return product(lhs, rhs, KB)

    def ag_start(src, dst, role, c):
        cols = pl.ds(c * CH, CH)
        for p, (o, n) in enumerate(PARTS):
            rows = pl.ds(o, n)
            remote(
                x.at[rows, cols] if src == 0 else xall.at[src - 1, 0, rows, cols],
                xall.at[dst - 1, 0, rows, cols],
                ag_send.at[dst - 1, c],
                ag_recv.at[dst - 1, c],
                nbr[p][role],
            ).start()

    def ag_arrived(n, c):
        await_bytes(xall.at[n - 1, 0, :, pl.ds(c * CH, CH)], ag_recv.at[n - 1, c])

    def pass_on(n, c):
        cols = pl.ds(c * CH, CH)
        if n < 2:
            dst = xbuf.at[n, pl.ds((1 - n) * ROWS, ROWS), cols]
        else:
            dst = xall.at[n - 1, 1, :, cols]
        src = x.at[:, cols] if n == 0 else xall.at[n - 1, 0, :, cols]
        remote(src, dst, ad_send.at[n, c], ad_recv.at[n, c], partner).start()

    def passed(n, c):
        await_bytes(x.at[:, pl.ds(0, CH)], ad_recv.at[n, c])

    def relay(n):
        for c in range(2):
            ag_arrived(n, c)
            pass_on(n, c)

    def x_load(n):
        xs = lax.rem(n, 2)
        return [
            local(xall.at[n - 1, 1 - h], xbuf.at[xs, pl.ds(h * ROWS, ROWS)], x_sem.at[h])
            for h in range(2)
        ]

    def own_load(c):
        cols = pl.ds(c * CH, CH)
        return local(xall.at[0, 0, :, cols], xbuf.at[1, pl.ds(ROWS, ROWS), cols], x_sem.at[c])

    def cols_of(j):
        return pl.ds(pl.multiple_of(j * V, T), V)

    def d2_start(n, j, slot):
        remote(
            d2s.at[slot],
            hub.at[2 + lax.rem(n, 2), :, cols_of(j)],
            ds_sem.at[slot],
            dr_sem.at[lax.rem(n, 2), j],
            partner,
        ).start()

    def d2_sent(slot):
        await_bytes(d2s.at[slot], ds_sem.at[slot])

    def d2_arrived(n, j):
        await_bytes(d2s.at[0], dr_sem.at[lax.rem(n, 2), j])

    def sum_start(n, j, role, dst):
        s = lax.rem(3 * (n - 1) + j, LS)
        for p, (o, rows) in enumerate(PARTS):
            to = nbr[p][C] if role is None else jnp.where(role, nbr[p][A], nbr[p][B])
            remote(
                ls.at[s, pl.ds(o, rows)],
                dst.at[pl.ds(o, rows), cols_of(j)],
                ls_sem.at[s],
                rs_recv.at[n - 1, j],
                to,
            ).start()

    def sum_on(n, j):
        sum_start(n, j, n < 5, rbuf.at[n - 1])

    def out_start(j):
        s = lax.rem(21 + j, LS)
        local(ls.at[s], y.at[:, cols_of(j)], ls_sem.at[s]).start()

    def sum_sent(g):
        s = lax.rem(g, LS)
        await_bytes(ls.at[s], ls_sem.at[s])

    def rs_arrived(n, j):
        await_bytes(d2s.at[0], rs_recv.at[n - 1, j])

    def term(n, cols, terms, v):
        v = v + hub[2 + lax.rem(n, 2), :, cols].astype(F32)
        for ref, r0 in terms:
            v = v + ref[pl.ds(r0, ROWS), cols].astype(F32)
        return v.astype(BF16)

    def add(n, j, terms, i):
        s = lax.rem(3 * (n - 1) + j, LS)
        cols = pl.ds(pl.multiple_of(j * V + i * T, T), T)
        ls[s, :, pl.ds(i * T, T)] = term(n, cols, terms, accbuf[:, cols])

    terms_c = ((xbuf.at[0], 0), (xbuf.at[1], ROWS))
    terms_0 = ((xbuf.at[0], ROWS), (xbuf.at[1], 0), (rlate, 0))

    def r_load(i, src, dst, col=0, width=D):
        cols = pl.ds(col, width)
        h, r = dst
        return local(rbuf.at[src - 1, :, cols], xbuf.at[h, pl.ds(r, ROWS), cols], r_sem.at[i])

    late_loads = (
        r_load(0, 3, (0, 0)), r_load(1, 6, (1, ROWS), 0, 2 * V), r_load(2, 6, (1, ROWS), 2 * V, V),
        r_load(3, 1, (0, ROWS)), r_load(4, 5, (1, 0)),
    )

    own = local(x, xbuf.at[0, pl.ds(0, ROWS)], x_sem.at[0])
    own.start()
    for i in range(3):
        for q, w in enumerate((wg, wu)):
            for d in range(2):
                local(
                    w.at[pl.ds(d * F, F), pl.ds(i * T, T)],
                    ring.at[q, :, pl.ds(d * W + i * T, T)],
                    f_sem.at[i],
                ).start()
    load_pair(1, 2)
    barrier = pltpu.get_barrier_semaphore()
    for d in (*axes, partner):
        pl.semaphore_signal(barrier, inc=1, device_id={"tp": d}, device_id_type=MESH)
    pl.semaphore_wait(barrier, 4)
    for c in range(2):
        pass_on(0, c)
    for c in range(2):
        ag_start(0, 1, A, c)
    rsum[...] = jnp.zeros_like(rsum)
    own.wait()

    def pieces(e):
        first = e == 0

        @_when(jnp.logical_not(first))
        def _():
            for q in range(2):
                chunk_wait(4 + q)
            load_pair(0, 6)

        def piece(m, _):
            h, i = m // 3, lax.rem(m, 3)

            @pl.when(first & (h == 0))
            def _():
                await_bytes(ring.at[0, :, pl.ds(0, 4 * T)], f_sem.at[i])

            @pl.when(first & (m == 3))
            def _():
                passed(0, 0)
                passed(0, 1)

            @_when(jnp.logical_not(first) & (i == 0))
            def _():
                for c in range(2):
                    @_when(m == 3 * c)
                    def _():
                        ag_arrived(1, c)
                        pass_on(1, c)
                        own_load(c).start()
                        ag_start(1, 2, B, c)
                        if c:
                            ag_start(1, 3, C, 0)
                            ag_start(1, 3, C, 1)

            tile_a(2 * e, 0, pl.multiple_of(h * ROWS, ROWS), i, 0, 1 - h, 3 * e + i)
            return 0

        lax.fori_loop(0, 6, piece, 0)

    def early(e, _):
        p = 2 * e
        chunk_wait(p)
        chunk_wait(p + 1)

        @_when(e < 5)
        def _():
            load_pair(lax.rem(e + 1, 3), p + 2)

        @_when(e >= 3)
        def _():
            @_when(e == 3)
            def _():
                for c in range(2):
                    passed(1, c)
                    own_load(c).wait()

            for c in range(2):
                @_when(e == 4 + c)
                def _():
                    ag_arrived(2, c)
                    pass_on(2, c)
                    ag_start(2, 4, C, c)
                    if c:
                        load_down(0, EARLY)
                        load_down(1, EARLY + 1)

        n = e // 3
        step_a(p, n, n, n == 0, lax.rem(e, 3))
        return 0

    def opening(g, _):
        pieces(2 * g)
        lax.fori_loop(2 * g + 1, 4 * g + 2, early, 0)
        return 0

    lax.fori_loop(0, 2, opening, 0)

    def block(n, _):
        base = EARLY + 9 * (n - 1)

        def down(j, _):
            p = base + j
            slot = lax.rem(n + j, 2)
            chunk_wait(p)

            @_when(j > 0)
            def _():
                d2_start(n, j - 1, 1 - slot)
                pl.when(j == 1)(lambda: load_one(wu, 0, p + 3))
                pl.when(j == 2)(lambda: load_one(wg, 1, p + 3))

            @pl.when((n > 1) | (j > 1))
            def _():
                d2_sent(slot)

            @_when(j == 0)
            def _():
                load_down(2, p + 2)
                load_one(wg, 0, p + 3)

                @_when(n > 1)
                def _():
                    sum_on(n - 1, 2)

                passed(n + 1, 0)
                passed(n + 1, 1)
                for copy in x_load(n + 1):
                    copy.start()

                for m, role in ((1, B), (3, C)):
                    @_when(n == m)
                    def _():
                        for c in range(2):
                            ag_start(0, m + 4, role, c)

                for m, blk in ((2, 4), (4, 6), (5, 7)):
                    _when(n == m)(functools.partial(relay, blk))

                for m, src in ((5, 2), (6, 4)):
                    @_when(n == m)
                    def _():
                        for i in range(3):
                            rs_arrived(src, i)
                        local(rbuf.at[src - 1], rsum, r_sem.at[0]).start()

            step_b(p, j, slot)
            return 0

        lax.fori_loop(0, 3, down, 0)

        def gate_up(j, _):
            p = base + 3 + 2 * j
            chunk_wait(p)
            chunk_wait(p + 1)

            @_when(j == 0)
            def _():
                d2_start(n, 2, lax.rem(n, 2))
                load_one(wu, 1, p + 3)
                for copy in x_load(n + 1):
                    copy.wait()

                @pl.when(n > 4)
                def _():
                    local(rbuf.at[0], rsum, r_sem.at[0]).wait()

                _when(n == 1)(lambda: relay(3))

                @_when(n == 2)
                def _():
                    relay(5)
                    for c in range(2):
                        ag_start(5, 6, C, c)

            @_when(j > 0)
            def _():
                sum_on(n, j - 1)
                _when(j == 1)(lambda: load_pair(2, p + 2))

                @_when(j == 2)
                def _():
                    for i in range(2):
                        load_down(i, p + 2 + i)

            @pl.when(3 * (n - 1) + j >= LS)
            def _():
                sum_sent(3 * (n - 1) + j)

            d2_arrived(n, j)

            def extra(i):
                for t in ((0, 1), (2,), (3,), (4,), (5,), ())[i]:
                    add(n, j, ((rsum, 0),), t)

            step_a(p, lax.rem(n + 1, 2), 1, False, j, extra)
            return 0

        lax.fori_loop(0, 3, gate_up, 0)
        return 0

    lax.fori_loop(1, 7, block, 0)

    def group(s, g, hb, h, store):
        for i in range(6):
            store(i, rows_b(hb, h, i, s))

    def on_c(j):
        sum_start(7, j, None, rlate)

    tops = (
        lambda: (sum_on(6, 2), load_down(2, FINAL + 2), chunk_wait(FINAL), d2_sent(0), d2_sent(1),
                 [rs_arrived(n, k) for n in (1, 3, 5) for k in range(3)], rs_arrived(6, 0), rs_arrived(6, 1),
                 [late_loads[i].start() for i in (0, 1, 3, 4)]),
        lambda: (d2_start(7, 0, 0), chunk_wait(FINAL + 1)),
        lambda: (d2_start(7, 1, 1), late_loads[0].wait(), late_loads[1].wait(), d2_arrived(7, 0), sum_sent(18)),
        lambda: (on_c(0), chunk_wait(FINAL + 2), d2_sent(0)),
        lambda: (d2_start(7, 2, 0), d2_arrived(7, 1), sum_sent(19), rs_arrived(6, 2), late_loads[2].start()),
        lambda: (on_c(1), d2_sent(1)),
        lambda: (d2_start(8, 0, 1), d2_arrived(7, 2), sum_sent(20), late_loads[2].wait()),
        lambda: (on_c(2), d2_sent(0)),
        lambda: (d2_start(8, 1, 0), d2_sent(1)),
        lambda: (d2_start(8, 2, 1), d2_arrived(8, 0), rs_arrived(7, 0), sum_sent(21), late_loads[3].wait(), late_loads[4].wait()),
        lambda: (out_start(0), d2_arrived(8, 1), rs_arrived(7, 1), sum_sent(22)),
    )

    def late(t, _):
        for lo, hi in ((0, 4), (4, 8), (8, 11)):
            @_when((t >= lo) & (t < hi))
            def _():
                for i in range(lo, hi):
                    _when(t == i)(tops[i])

        w_c = (t == 2) | (t == 4) | (t == 6)
        w_0 = t > 8
        o = jnp.where(t < 2, t, jnp.where(t == 3, 2, jnp.where(t == 5, 3, t - 3)))
        g = jnp.where(w_c, t // 2 - 1, jnp.where(w_0, t - 9, lax.rem(o, 3)))
        s = lax.rem(FINAL + g, RING)

        @pl.when(jnp.logical_not(w_c | w_0))
        def _():
            def store(i, v):
                d2s[lax.rem(o, 2), :, pl.ds(i * T, T)] = v.astype(BF16)

            group(s, g, jnp.where(o < 3, 1, 0), 0, store)

        for cond, n, terms in ((w_c, 7, terms_c), (w_0, 8, terms_0)):
            @pl.when(cond)
            def _():
                def store(i, v):
                    cols = pl.ds(pl.multiple_of(g * V + i * T, T), T)
                    ls[lax.rem(3 * (n - 1) + g, LS), :, pl.ds(i * T, T)] = term(n, cols, terms, v)

                group(s, g, 8 - n, 1, store)

        return 0

    lax.fori_loop(0, 11, late, 0)

    last = 2
    out_start(1)
    sum_sent(23)
    d2_arrived(8, last)

    def keep(i, v):
        cols = pl.ds(last * V + i * T, T)
        accbuf[:, cols] = v

    group((FINAL + last) % RING, last, 0, 1, keep)
    rs_arrived(7, last)
    for i in range(6):
        add(8, last, terms_0, i)
    out_start(last)

    for s in range(LS):
        sum_sent(s)
    d2_sent(0)
    d2_sent(1)
    for c in range(2):
        for n in range(8):
            await_bytes(x.at[:, pl.ds(0, CH)], ad_send.at[n, c])
            if n:
                await_bytes(x.at[:, pl.ds(0, CH)], ag_send.at[n - 1, c])


def _call(x, wg, wu, wd):
    dma = pltpu.SemaphoreType.DMA
    rows = (ROWS, D)
    return pl.pallas_call(
        _kernel,
        out_shape=tuple(
            jax.ShapeDtypeStruct(shape, BF16) for shape in (rows, (7, 2, *rows), (6, *rows))
        ),
        in_specs=[pl.BlockSpec(memory_space=pltpu.HBM)] * 4,
        out_specs=[pl.BlockSpec(memory_space=pltpu.HBM)] * 3,
        scratch_shapes=[
            pltpu.VMEM((2, 2 * ROWS, D), BF16),
            pltpu.VMEM((4, *rows), BF16),
            pltpu.VMEM((RING, F, V), BF16),
            pltpu.VMEM(rows, F32),
            pltpu.VMEM((2, ROWS, V), BF16),
            pltpu.VMEM((LS, ROWS, V), BF16),
            pltpu.VMEM(rows, BF16),
            pltpu.VMEM(rows, BF16),
            *(dma(s) for s in ((RING,), (3,), (2,), (5,), (7, 2), (7, 2), (8, 2), (8, 2), (2,), (2, 3), (LS,), (7, 3))),
        ],
        compiler_params=pltpu.CompilerParams(
            collective_id=0, has_side_effects=True, vmem_limit_bytes=67_000_000
        ),
        name="mlp",
    )(x, wg, wu, wd)[0]


def solution(mesh):
    return jax.shard_map(
        _call,
        mesh=mesh,
        in_specs=(P(("dp", "tp"), None), P(None, "tp"), P(None, "tp"), P("tp", None)),
        out_specs=P(("dp", "tp"), None),
        check_vma=False,
    )
```

time: 317 us -> 304 us (0.959)
  Pallas kernels: 314 us -> 300 us
    pallas_call x1, Pallas kernels: 314 us -> 300 us  [_call(): pl.pallas_call(_kernel, out_shape=tuple((jax.ShapeDtypeStruct(shape, BF16...]
where the time goes in v3:
time: 304 us
  Pallas kernels  300 us (99%)
  local copies, waits for them, and re-layouts  3.22 us (1%)
    pallas_call x1, Pallas kernels, _call(): pl.pallas_call(_kernel, out_shape=tuple((jax.ShapeDtypeStruct(shape, BF16...  300 us

profile of v3, /device:TPU:0, one launch (start us, length us, event | category | flops | bytes accessed | tf_op | source)
XLA Modules:
  0.0 303.5 jit_solution(6290081911593424735)
XLA Ops:
  0.0 300.3 %mlp.1 = (bf16[256,4608]{1,0:T(8,128)(2,1)}, bf16[7,2,256,4608]{3,2,1,0:T(8,128)(2,1)}, bf16[6,256,4608]{2,1,0:T(8,128)(2,1)}) custom-call(bf16[256,4608]{1,0:T(8,128)(2,1)} %x.1, bf16[4608,2304]{1,0:T(8,128)(2,1)} %wg.1, bf16[4608,2304]{1,0:T(8,128)(2,1)} %wu.1, bf16[2304,4608]{1,0:T(8,128)(2,1)} %wd.1), custom_call_target="tpu_custom_call" | custom-call | tf_op jit(solution)/shard_map/mlp/pallas_call | solution.py:536
  300.3 3.2 %copy.6 = bf16[256,4608]{1,0:T(8,128)(2,1)} copy(bf16[256,4608]{1,0:T(8,128)(2,1)} %get-tuple-element.6) | data formatting | bytes 4718592

commit v4 on v3

--- a/solution.py
+++ b/solution.py
@@ -23,6 +23,7 @@
 EARLY = 12
 FINAL = 66
 LS = 4
+SLICE = 16
 A, B, C = range(3)
 
 
@@ -45,7 +46,7 @@
 def _kernel(
     x, wg, wu, wd, y, xall, rbuf,
     xbuf, hub, ring, accbuf, d2s, ls, rsum, rlate,
-    w_sem, f_sem, x_sem, r_sem, ag_send, ag_recv, ad_send, ad_recv, ds_sem, dr_sem, ls_sem, rs_recv,
+    w_sem, f_sem, x_sem, r_sem, ag_send, ag_recv, ad_recv, ds_sem, dr_sem, ls_sem, rs_recv,
 ):
     me = lax.axis_index("tp")
     core = lax.rem(me, 2)
@@ -95,7 +96,7 @@
             total = t if total is None else total + t
         return total
 
-    def tile_a(p, xs, row, i, hb, half, j):
+    def tile_a(p, xs, row, i, hb, half, j, extra=None):
         sl = [lax.rem(p + q, RING) for q in range(2)]
 
         def lhs(k):
@@ -109,14 +110,18 @@
             return tile
 
         g, u = product(lhs, rhs(0), KA), product(lhs, rhs(1), KA)
-        hub[hb, :, pl.ds(pl.multiple_of(half * F + j * T, T), T)] = _gelu_mul(g, u)
+        cols = pl.ds(pl.multiple_of(half * F + j * T, T), T)
+        if extra is not None:
+            extra()
+        hub[hb, :, cols] = _gelu_mul(g, u)
 
     def step_a(p, xs, hb, flip, e, extra=None):
         for i in range(3):
             for h in range(2):
-                tile_a(p, xs, h * ROWS, i, hb, jnp.where(flip, 1 - h, h), 3 * e + i)
-                if extra is not None:
-                    extra(2 * i + h)
+                tile_a(
+                    p, xs, h * ROWS, i, hb, jnp.where(flip, 1 - h, h), 3 * e + i,
+                    extra and functools.partial(extra, 2 * i + h),
+                )
 
     def step_b(p, j, slot):
         s = lax.rem(p, RING)
@@ -140,7 +145,7 @@
             remote(
                 x.at[rows, cols] if src == 0 else xall.at[src - 1, 0, rows, cols],
                 xall.at[dst - 1, 0, rows, cols],
-                ag_send.at[dst - 1, c],
+                ag_send.at[0],
                 ag_recv.at[dst - 1, c],
                 nbr[p][role],
             ).start()
@@ -155,7 +160,7 @@
         else:
             dst = xall.at[n - 1, 1, :, cols]
         src = x.at[:, cols] if n == 0 else xall.at[n - 1, 0, :, cols]
-        remote(src, dst, ad_send.at[n, c], ad_recv.at[n, c], partner).start()
+        remote(src, dst, ag_send.at[1], ad_recv.at[n, c], partner).start()
 
     def passed(n, c):
         await_bytes(x.at[:, pl.ds(0, CH)], ad_recv.at[n, c])
@@ -220,16 +225,17 @@
     def rs_arrived(n, j):
         await_bytes(d2s.at[0], rs_recv.at[n - 1, j])
 
-    def term(n, cols, terms, v):
-        v = v + hub[2 + lax.rem(n, 2), :, cols].astype(F32)
-        for ref, r0 in terms:
-            v = v + ref[pl.ds(r0, ROWS), cols].astype(F32)
-        return v.astype(BF16)
-
-    def add(n, j, terms, i):
+    def add(n, j, terms, i, value=None):
         s = lax.rem(3 * (n - 1) + j, LS)
         cols = pl.ds(pl.multiple_of(j * V + i * T, T), T)
-        ls[s, :, pl.ds(i * T, T)] = term(n, cols, terms, accbuf[:, cols])
+        size = SLICE if value is None else ROWS
+        for r in range(0, ROWS, size):
+            rows = pl.ds(r, size)
+            v = accbuf[rows, cols] if value is None else value
+            v = v + hub[2 + lax.rem(n, 2), rows, cols].astype(F32)
+            for ref, r0 in terms:
+                v = v + ref[pl.ds(r0 + r, size), cols].astype(F32)
+            ls[s, rows, pl.ds(i * T, T)] = v.astype(BF16)
 
     terms_c = ((xbuf.at[0], 0), (xbuf.at[1], ROWS))
     terms_0 = ((xbuf.at[0], ROWS), (xbuf.at[1], 0), (rlate, 0))
@@ -240,13 +246,11 @@
         return local(rbuf.at[src - 1, :, cols], xbuf.at[h, pl.ds(r, ROWS), cols], r_sem.at[i])
 
     late_loads = (
-        r_load(0, 3, (0, 0)), r_load(1, 6, (1, ROWS), 0, 2 * V), r_load(2, 6, (1, ROWS), 2 * V, V),
-        r_load(3, 1, (0, ROWS)), r_load(4, 5, (1, 0)),
+        r_load(0, 3, (0, 0)), *(r_load(1 + k, 6, (1, ROWS), k * V, V) for k in range(3)),
+        r_load(4, 1, (0, ROWS)), r_load(5, 5, (1, 0)),
     )
 
-    own = local(x, xbuf.at[0, pl.ds(0, ROWS)], x_sem.at[0])
-    own.start()
-    for i in range(3):
+    def first_tile(i):
         for q, w in enumerate((wg, wu)):
             for d in range(2):
                 local(
@@ -254,56 +258,66 @@
                     ring.at[q, :, pl.ds(d * W + i * T, T)],
                     f_sem.at[i],
                 ).start()
-    load_pair(1, 2)
+
+    own = local(x, xbuf.at[0, pl.ds(0, ROWS)], x_sem.at[0])
+    own.start()
+    first_tile(0)
     barrier = pltpu.get_barrier_semaphore()
     for d in (*axes, partner):
         pl.semaphore_signal(barrier, inc=1, device_id={"tp": d}, device_id_type=MESH)
+    rsum[...] = jnp.zeros_like(rsum)
+    first_tile(1)
     pl.semaphore_wait(barrier, 4)
     for c in range(2):
         pass_on(0, c)
     for c in range(2):
         ag_start(0, 1, A, c)
-    rsum[...] = jnp.zeros_like(rsum)
     own.wait()
 
-    def pieces(e):
-        first = e == 0
-
-        @_when(jnp.logical_not(first))
+    def piece(i, _):
+        await_bytes(ring.at[0, :, pl.ds(0, 4 * T)], f_sem.at[i])
+        _when(i == 0)(lambda: first_tile(2))
+        _when(i == 1)(lambda: load_pair(1, 2))
+        tile_a(0, 0, 0, i, 0, 1, i)
+        return 0
+
+    lax.fori_loop(0, 3, piece, 0)
+
+    def third(m, _):
+        @_when(m == 0)
         def _():
-            for q in range(2):
-                chunk_wait(4 + q)
-            load_pair(0, 6)
-
-        def piece(m, _):
-            h, i = m // 3, lax.rem(m, 3)
-
-            @pl.when(first & (h == 0))
-            def _():
-                await_bytes(ring.at[0, :, pl.ds(0, 4 * T)], f_sem.at[i])
-
-            @pl.when(first & (m == 3))
-            def _():
-                passed(0, 0)
-                passed(0, 1)
-
-            @_when(jnp.logical_not(first) & (i == 0))
-            def _():
-                for c in range(2):
-                    @_when(m == 3 * c)
-                    def _():
-                        ag_arrived(1, c)
-                        pass_on(1, c)
-                        own_load(c).start()
-                        ag_start(1, 2, B, c)
-                        if c:
-                            ag_start(1, 3, C, 0)
-                            ag_start(1, 3, C, 1)
-
+            passed(0, 0)
+            passed(0, 1)
+
+        @_when(m > 0)
+        def _():
+            @_when(m == 1)
+            def _():
+                for q in range(2):
+                    chunk_wait(4 + q)
+                load_pair(0, 6)
+
+            for c in range(2):
+                @_when(m == 1 + c)
+                def _():
+                    ag_arrived(1, c)
+                    pass_on(1, c)
+                    own_load(c).start()
+                    ag_start(1, 2, B, c)
+                    if c:
+                        ag_start(1, 3, C, 0)
+                        ag_start(1, 3, C, 1)
+
+        h = jnp.where(m == 1, 0, 1)
+        e = jnp.where(m == 0, 0, 2)
+        for i in range(3):
             tile_a(2 * e, 0, pl.multiple_of(h * ROWS, ROWS), i, 0, 1 - h, 3 * e + i)
-            return 0
-
-        lax.fori_loop(0, 6, piece, 0)
+        return 0
+
+    def third_hop(c):
+        ag_arrived(2, c)
+        pass_on(2, c)
+        ag_start(2, 4, C, c)
 
     def early(e, _):
         p = 2 * e
@@ -322,22 +336,19 @@
                     passed(1, c)
                     own_load(c).wait()
 
-            for c in range(2):
-                @_when(e == 4 + c)
-                def _():
-                    ag_arrived(2, c)
-                    pass_on(2, c)
-                    ag_start(2, 4, C, c)
-                    if c:
-                        load_down(0, EARLY)
-                        load_down(1, EARLY + 1)
+            _when(e == 4)(lambda: third_hop(0))
+
+            @_when(e == 5)
+            def _():
+                for i in range(2):
+                    load_down(i, EARLY + i)
 
         n = e // 3
         step_a(p, n, n, n == 0, lax.rem(e, 3))
         return 0
 
     def opening(g, _):
-        pieces(2 * g)
+        lax.fori_loop(g, 2 * g + 1, third, 0)
         lax.fori_loop(2 * g + 1, 4 * g + 2, early, 0)
         return 0
 
@@ -354,8 +365,15 @@
             @_when(j > 0)
             def _():
                 d2_start(n, j - 1, 1 - slot)
-                pl.when(j == 1)(lambda: load_one(wu, 0, p + 3))
-                pl.when(j == 2)(lambda: load_one(wg, 1, p + 3))
+                _when(j == 2)(lambda: load_one(wg, 1, p + 3))
+
+                @_when(j == 1)
+                def _():
+                    load_one(wu, 0, p + 3)
+                    passed(n + 1, 0)
+                    passed(n + 1, 1)
+                    for copy in x_load(n + 1):
+                        copy.start()
 
             @pl.when((n > 1) | (j > 1))
             def _():
@@ -370,10 +388,7 @@
                 def _():
                     sum_on(n - 1, 2)
 
-                passed(n + 1, 0)
-                passed(n + 1, 1)
-                for copy in x_load(n + 1):
-                    copy.start()
+                _when(n == 1)(lambda: third_hop(1))
 
                 for m, role in ((1, B), (3, C)):
                     @_when(n == m)
@@ -455,19 +470,23 @@
     def on_c(j):
         sum_start(7, j, None, rlate)
 
+    def r_due(k):
+        rs_arrived(6, k)
+        late_loads[1 + k].start()
+
     tops = (
         lambda: (sum_on(6, 2), load_down(2, FINAL + 2), chunk_wait(FINAL), d2_sent(0), d2_sent(1),
-                 [rs_arrived(n, k) for n in (1, 3, 5) for k in range(3)], rs_arrived(6, 0), rs_arrived(6, 1),
-                 [late_loads[i].start() for i in (0, 1, 3, 4)]),
+                 [rs_arrived(n, k) for n in (1, 3, 5) for k in range(3)], r_due(0),
+                 [late_loads[i].start() for i in (0, 4, 5)]),
         lambda: (d2_start(7, 0, 0), chunk_wait(FINAL + 1)),
-        lambda: (d2_start(7, 1, 1), late_loads[0].wait(), late_loads[1].wait(), d2_arrived(7, 0), sum_sent(18)),
+        lambda: (d2_start(7, 1, 1), late_loads[0].wait(), late_loads[1].wait(), d2_arrived(7, 0), sum_sent(18), r_due(1)),
         lambda: (on_c(0), chunk_wait(FINAL + 2), d2_sent(0)),
-        lambda: (d2_start(7, 2, 0), d2_arrived(7, 1), sum_sent(19), rs_arrived(6, 2), late_loads[2].start()),
-        lambda: (on_c(1), d2_sent(1)),
-        lambda: (d2_start(8, 0, 1), d2_arrived(7, 2), sum_sent(20), late_loads[2].wait()),
-        lambda: (on_c(2), d2_sent(0)),
-        lambda: (d2_start(8, 1, 0), d2_sent(1)),
-        lambda: (d2_start(8, 2, 1), d2_arrived(8, 0), rs_arrived(7, 0), sum_sent(21), late_loads[3].wait(), late_loads[4].wait()),
+        lambda: (d2_start(7, 2, 0), d2_arrived(7, 1), sum_sent(19), late_loads[2].wait()),
+        lambda: (on_c(1), d2_sent(1), r_due(2)),
+        lambda: (d2_start(8, 0, 1), d2_arrived(7, 2), sum_sent(20), late_loads[3].wait()),
+        lambda: d2_sent(0),
+        lambda: (d2_start(8, 1, 0), d2_sent(1), on_c(2)),
+        lambda: (d2_start(8, 2, 1), d2_arrived(8, 0), rs_arrived(7, 0), sum_sent(21), late_loads[4].wait(), late_loads[5].wait()),
         lambda: (out_start(0), d2_arrived(8, 1), rs_arrived(7, 1), sum_sent(22)),
     )
 
@@ -494,11 +513,7 @@
         for cond, n, terms in ((w_c, 7, terms_c), (w_0, 8, terms_0)):
             @pl.when(cond)
             def _():
-                def store(i, v):
-                    cols = pl.ds(pl.multiple_of(g * V + i * T, T), T)
-                    ls[lax.rem(3 * (n - 1) + g, LS), :, pl.ds(i * T, T)] = term(n, cols, terms, v)
-
-                group(s, g, 8 - n, 1, store)
+                group(s, g, 8 - n, 1, lambda i, v: add(n, g, terms, i, v))
 
         return 0
 
@@ -515,25 +530,41 @@
 
     group((FINAL + last) % RING, last, 0, 1, keep)
     rs_arrived(7, last)
-    for i in range(6):
-        add(8, last, terms_0, i)
-    out_start(last)
-
+    for half in range(2):
+        for i in range(3):
+            add(8, last, terms_0, 3 * half + i)
+        lo = half * W
+        local(
+            ls.at[23 % LS, :, pl.ds(lo, W)], y.at[:, pl.ds(last * V + lo, W)], ls_sem.at[23 % LS]
+        ).start()
+
+    d2_sent(0)
+    d2_sent(1)
+    await_bytes(xall.at[:, 0], ag_send.at[0])
+    await_bytes(xall.at[pl.ds(0, 4)], ag_send.at[1])
     for s in range(LS):
         sum_sent(s)
-    d2_sent(0)
-    d2_sent(1)
-    for c in range(2):
-        for n in range(8):
-            await_bytes(x.at[:, pl.ds(0, CH)], ad_send.at[n, c])
-            if n:
-                await_bytes(x.at[:, pl.ds(0, CH)], ag_send.at[n - 1, c])
+
+
+def _copy(src, dst, buf, get, put):
+    n = get.shape[0]
+    step = ROWS // n
+    rows = [pl.ds(i * step, step) for i in range(n)]
+    gets = [pltpu.make_async_copy(src.at[r], buf.at[r], get.at[i]) for i, r in enumerate(rows)]
+    puts = [pltpu.make_async_copy(buf.at[r], dst.at[r], put.at[i]) for i, r in enumerate(rows)]
+    for g in gets:
+        g.start()
+    for g, p in zip(gets, puts):
+        g.wait()
+        p.start()
+    for p in puts:
+        p.wait()
 
 
 def _call(x, wg, wu, wd):
     dma = pltpu.SemaphoreType.DMA
     rows = (ROWS, D)
-    return pl.pallas_call(
+    out = pl.pallas_call(
         _kernel,
         out_shape=tuple(
             jax.ShapeDtypeStruct(shape, BF16) for shape in (rows, (7, 2, *rows), (6, *rows))
@@ -549,13 +580,21 @@
             pltpu.VMEM((LS, ROWS, V), BF16),
             pltpu.VMEM(rows, BF16),
             pltpu.VMEM(rows, BF16),
-            *(dma(s) for s in ((RING,), (3,), (2,), (5,), (7, 2), (7, 2), (8, 2), (8, 2), (2,), (2, 3), (LS,), (7, 3))),
+            *(dma(s) for s in ((RING,), (3,), (2,), (6,), (2,), (7, 2), (8, 2), (2,), (2, 3), (LS,), (7, 3))),
         ],
         compiler_params=pltpu.CompilerParams(
             collective_id=0, has_side_effects=True, vmem_limit_bytes=67_000_000
         ),
         name="mlp",
     )(x, wg, wu, wd)[0]
+    return pl.pallas_call(
+        _copy,
+        out_shape=jax.ShapeDtypeStruct(rows, BF16),
+        in_specs=[pl.BlockSpec(memory_space=pltpu.HBM)],
+        out_specs=pl.BlockSpec(memory_space=pltpu.HBM),
+        scratch_shapes=[pltpu.VMEM(rows, BF16), dma((8,)), dma((8,))],
+        name="hand_over",
+    )(out)
 
 
 def solution(mesh):

time: 304 us -> 294 us (0.967)
  Pallas kernels: 300 us -> 294 us
  local copies, waits for them, and re-layouts: 3.22 us -> 0 us
    pallas_call x1, Pallas kernels: 300 us -> 292 us  [_call(): pl.pallas_call(_kernel, out_shape=tuple((jax.ShapeDtypeStruct(shape, BF16...]
    unnamed x1 -> x0, local copies, waits for them, and re-layouts: 3.22 us -> none
where the time goes in v4:
time: 294 us
  Pallas kernels  294 us (100%)
    pallas_call x1, Pallas kernels, _call(): pl.pallas_call(_kernel, out_shape=tuple((jax.ShapeDtypeStruct(shape, BF16...  292 us

profile of v4, /device:TPU:0, one launch (start us, length us, event | category | flops | bytes accessed | tf_op | source)
XLA Modules:
  0.0 294.3 jit_solution(1280182098446034375)
XLA Ops:
  0.0 291.7 %mlp.1 = (bf16[256,4608]{1,0:T(8,128)(2,1)}, bf16[7,2,256,4608]{3,2,1,0:T(8,128)(2,1)}, bf16[6,256,4608]{2,1,0:T(8,128)(2,1)}) custom-call(bf16[256,4608]{1,0:T(8,128)(2,1)} %x.1, bf16[4608,2304]{1,0:T(8,128)(2,1)} %wg.1, bf16[4608,2304]{1,0:T(8,128)(2,1)} %wu.1, bf16[2304,4608]{1,0:T(8,128)(2,1)} %wd.1), custom_call_target="tpu_custom_call" | custom-call | tf_op jit(solution)/shard_map/mlp/pallas_call | solution.py:567
  291.7 2.5 hand_over.1

commit v5 on v4

--- a/solution.py
+++ b/solution.py
@@ -45,7 +45,7 @@
 
 def _kernel(
     x, wg, wu, wd, y, xall, rbuf,
-    xbuf, hub, ring, accbuf, d2s, ls, rsum, rlate,
+    xbuf, hub, ring, accbuf, d2s, ls, rsum, rlate, pair,
     w_sem, f_sem, x_sem, r_sem, ag_send, ag_recv, ad_recv, ds_sem, dr_sem, ls_sem, rs_recv,
 ):
     me = lax.axis_index("tp")
@@ -111,9 +111,14 @@
 
         g, u = product(lhs, rhs(0), KA), product(lhs, rhs(1), KA)
         cols = pl.ds(pl.multiple_of(half * F + j * T, T), T)
-        if extra is not None:
-            extra()
-        hub[hb, :, cols] = _gelu_mul(g, u)
+        if extra is None:
+            hub[hb, :, cols] = _gelu_mul(g, u)
+            return
+        pair[0], pair[1] = g, u
+        for r in range(0, ROWS, SLICE):
+            rows = pl.ds(r, SLICE)
+            extra(r)
+            hub[hb, rows, cols] = _gelu_mul(pair[0, rows], pair[1, rows])
 
     def step_a(p, xs, hb, flip, e, extra=None):
         for i in range(3):
@@ -214,10 +219,6 @@
     def sum_on(n, j):
         sum_start(n, j, n < 5, rbuf.at[n - 1])
 
-    def out_start(j):
-        s = lax.rem(21 + j, LS)
-        local(ls.at[s], y.at[:, cols_of(j)], ls_sem.at[s]).start()
-
     def sum_sent(g):
         s = lax.rem(g, LS)
         await_bytes(ls.at[s], ls_sem.at[s])
@@ -225,17 +226,22 @@
     def rs_arrived(n, j):
         await_bytes(d2s.at[0], rs_recv.at[n - 1, j])
 
+    def add_rows(n, j, terms, i, r, value=None):
+        size = SLICE if value is None else ROWS
+        cols = pl.ds(pl.multiple_of(j * V + i * T, T), T)
+        rows = pl.ds(r, size)
+        v = accbuf[rows, cols] if value is None else value
+        v = v + hub[2 + lax.rem(n, 2), rows, cols].astype(F32)
+        for ref, r0 in terms:
+            v = v + ref[pl.ds(r0 + r, size), cols].astype(F32)
+        if isinstance(n, int) and n == 8:
+            y[rows, cols] = v.astype(BF16)
+        else:
+            ls[lax.rem(3 * (n - 1) + j, LS), rows, pl.ds(i * T, T)] = v.astype(BF16)
+
     def add(n, j, terms, i, value=None):
-        s = lax.rem(3 * (n - 1) + j, LS)
-        cols = pl.ds(pl.multiple_of(j * V + i * T, T), T)
-        size = SLICE if value is None else ROWS
-        for r in range(0, ROWS, size):
-            rows = pl.ds(r, size)
-            v = accbuf[rows, cols] if value is None else value
-            v = v + hub[2 + lax.rem(n, 2), rows, cols].astype(F32)
-            for ref, r0 in terms:
-                v = v + ref[pl.ds(r0 + r, size), cols].astype(F32)
-            ls[s, rows, pl.ds(i * T, T)] = v.astype(BF16)
+        for r in range(0, ROWS, SLICE if value is None else ROWS):
+            add_rows(n, j, terms, i, r, value)
 
     terms_c = ((xbuf.at[0], 0), (xbuf.at[1], ROWS))
     terms_0 = ((xbuf.at[0], ROWS), (xbuf.at[1], 0), (rlate, 0))
@@ -451,9 +457,12 @@
 
             d2_arrived(n, j)
 
-            def extra(i):
-                for t in ((0, 1), (2,), (3,), (4,), (5,), ())[i]:
-                    add(n, j, ((rsum, 0),), t)
+            def extra(i, r):
+                q = (i * ROWS + r) // SLICE
+                for k in range(6 * q // 5, 6 * (q + 1) // 5):
+                    t, row = divmod(k * SLICE, ROWS)
+                    if t < 6:
+                        add_rows(n, j, ((rsum, 0),), t, row)
 
             step_a(p, lax.rem(n + 1, 2), 1, False, j, extra)
             return 0
@@ -486,8 +495,8 @@
         lambda: (d2_start(8, 0, 1), d2_arrived(7, 2), sum_sent(20), late_loads[3].wait()),
         lambda: d2_sent(0),
         lambda: (d2_start(8, 1, 0), d2_sent(1), on_c(2)),
-        lambda: (d2_start(8, 2, 1), d2_arrived(8, 0), rs_arrived(7, 0), sum_sent(21), late_loads[4].wait(), late_loads[5].wait()),
-        lambda: (out_start(0), d2_arrived(8, 1), rs_arrived(7, 1), sum_sent(22)),
+        lambda: (d2_start(8, 2, 1), d2_arrived(8, 0), rs_arrived(7, 0), late_loads[4].wait(), late_loads[5].wait()),
+        lambda: (d2_arrived(8, 1), rs_arrived(7, 1)),
     )
 
     def late(t, _):
@@ -520,8 +529,6 @@
     lax.fori_loop(0, 11, late, 0)
 
     last = 2
-    out_start(1)
-    sum_sent(23)
     d2_arrived(8, last)
 
     def keep(i, v):
@@ -530,13 +537,8 @@
 
     group((FINAL + last) % RING, last, 0, 1, keep)
     rs_arrived(7, last)
-    for half in range(2):
-        for i in range(3):
-            add(8, last, terms_0, 3 * half + i)
-        lo = half * W
-        local(
-            ls.at[23 % LS, :, pl.ds(lo, W)], y.at[:, pl.ds(last * V + lo, W)], ls_sem.at[23 % LS]
-        ).start()
+    for i in range(6):
+        add(8, last, terms_0, i)
 
     d2_sent(0)
     d2_sent(1)
@@ -546,31 +548,17 @@
         sum_sent(s)
 
 
-def _copy(src, dst, buf, get, put):
-    n = get.shape[0]
-    step = ROWS // n
-    rows = [pl.ds(i * step, step) for i in range(n)]
-    gets = [pltpu.make_async_copy(src.at[r], buf.at[r], get.at[i]) for i, r in enumerate(rows)]
-    puts = [pltpu.make_async_copy(buf.at[r], dst.at[r], put.at[i]) for i, r in enumerate(rows)]
-    for g in gets:
-        g.start()
-    for g, p in zip(gets, puts):
-        g.wait()
-        p.start()
-    for p in puts:
-        p.wait()
-
-
 def _call(x, wg, wu, wd):
     dma = pltpu.SemaphoreType.DMA
     rows = (ROWS, D)
-    out = pl.pallas_call(
+    return pl.pallas_call(
         _kernel,
-        out_shape=tuple(
-            jax.ShapeDtypeStruct(shape, BF16) for shape in (rows, (7, 2, *rows), (6, *rows))
+        out_shape=(
+            pltpu.VMEM(rows, BF16),
+            *(pltpu.HBM(shape, BF16) for shape in ((7, 2, *rows), (6, *rows))),
         ),
         in_specs=[pl.BlockSpec(memory_space=pltpu.HBM)] * 4,
-        out_specs=[pl.BlockSpec(memory_space=pltpu.HBM)] * 3,
+        out_specs=[pl.BlockSpec(memory_space=m) for m in (pltpu.VMEM, pltpu.HBM, pltpu.HBM)],
         scratch_shapes=[
             pltpu.VMEM((2, 2 * ROWS, D), BF16),
             pltpu.VMEM((4, *rows), BF16),
@@ -580,21 +568,14 @@
             pltpu.VMEM((LS, ROWS, V), BF16),
             pltpu.VMEM(rows, BF16),
             pltpu.VMEM(rows, BF16),
+            pltpu.VMEM((2, ROWS, T), F32),
             *(dma(s) for s in ((RING,), (3,), (2,), (6,), (2,), (7, 2), (8, 2), (2,), (2, 3), (LS,), (7, 3))),
         ],
         compiler_params=pltpu.CompilerParams(
-            collective_id=0, has_side_effects=True, vmem_limit_bytes=67_000_000
+            collective_id=0, has_side_effects=True, vmem_limit_bytes=64_500_000
         ),
         name="mlp",
     )(x, wg, wu, wd)[0]
-    return pl.pallas_call(
-        _copy,
-        out_shape=jax.ShapeDtypeStruct(rows, BF16),
-        in_specs=[pl.BlockSpec(memory_space=pltpu.HBM)],
-        out_specs=pl.BlockSpec(memory_space=pltpu.HBM),
-        scratch_shapes=[pltpu.VMEM(rows, BF16), dma((8,)), dma((8,))],
-        name="hand_over",
-    )(out)
 
 
 def solution(mesh):

time: 294 us -> 290 us (0.986)
  Pallas kernels: 294 us -> 288 us
    pallas_call x2 -> x1, Pallas kernels: 294 us -> 288 us  [_call(): pl.pallas_call(_kernel, out_shape=(pltpu.VMEM(rows, BF16), *(pltpu.HBM(sh...]
where the time goes in v5:
time: 290 us
  Pallas kernels  288 us (99%)
    pallas_call x1, Pallas kernels, _call(): pl.pallas_call(_kernel, out_shape=(pltpu.VMEM(rows, BF16), *(pltpu.HBM(sh...  288 us

profile of v5, /device:TPU:0, one launch (start us, length us, event | category | flops | bytes accessed | tf_op | source)
XLA Modules:
  0.0 289.7 jit_solution(3278352774074756959)
XLA Ops:
  0.0 288.3 %mlp.1 = (bf16[256,4608]{1,0:T(8,128)(2,1)S(1)}, bf16[7,2,256,4608]{3,2,1,0:T(8,128)(2,1)}, bf16[6,256,4608]{2,1,0:T(8,128)(2,1)}) custom-call(bf16[256,4608]{1,0:T(8,128)(2,1)} %x.1, bf16[4608,2304]{1,0:T(8,128)(2,1)} %wg.1, bf16[4608,2304]{1,0:T(8,128)(2,1)} %wu.1, bf16[2304,4608]{1,0:T(8,128)(2,1)} %wd.1), custom_call_target="tpu_custom_call" | custom-call | tf_op jit(solution)/shard_map/mlp/pallas_call | solution.py:554
  288.3 1.4 copy.6

commit v6 on v5

--- a/solution.py
+++ b/solution.py
@@ -22,7 +22,7 @@
 RING = 4
 EARLY = 12
 FINAL = 66
-LS = 4
+LS = 2
 SLICE = 16
 A, B, C = range(3)
 
@@ -45,7 +45,7 @@
 
 def _kernel(
     x, wg, wu, wd, y, xall, rbuf,
-    xbuf, hub, ring, accbuf, d2s, ls, rsum, rlate, pair,
+    xbuf, hub, ring, accbuf, d2s, pair,
     w_sem, f_sem, x_sem, r_sem, ag_send, ag_recv, ad_recv, ds_sem, dr_sem, ls_sem, rs_recv,
 ):
     me = lax.axis_index("tp")
@@ -204,47 +204,46 @@
     def d2_arrived(n, j):
         await_bytes(d2s.at[0], dr_sem.at[lax.rem(n, 2), j])
 
-    def sum_start(n, j, role, dst):
-        s = lax.rem(3 * (n - 1) + j, LS)
+    def out_at(h, rows, col, width):
+        return 4, rows, pl.ds(pl.multiple_of(h * CH + col, T), width)
+
+    def sum_start(n, j, to, src, sem, width, dst):
+        cols = pl.ds(pl.multiple_of(j * width, T), width)
         for p, (o, rows) in enumerate(PARTS):
-            to = nbr[p][C] if role is None else jnp.where(role, nbr[p][A], nbr[p][B])
             remote(
-                ls.at[s, pl.ds(o, rows)],
-                dst.at[pl.ds(o, rows), cols_of(j)],
-                ls_sem.at[s],
+                src(pl.ds(o, rows)),
+                dst.at[pl.ds(o, rows), cols],
+                sem,
                 rs_recv.at[n - 1, j],
-                to,
+                to(p),
             ).start()
 
-    def sum_on(n, j):
-        sum_start(n, j, n < 5, rbuf.at[n - 1])
-
-    def sum_sent(g):
-        s = lax.rem(g, LS)
-        await_bytes(ls.at[s], ls_sem.at[s])
+    def sum_on(n, h):
+        sum_start(
+            n, h, lambda p: jnp.where(n < 5, nbr[p][A], nbr[p][B]),
+            lambda rows: hub.at[out_at(h, rows, 0, CH)], ls_sem.at[h], CH, rbuf.at[n - 1],
+        )
+
+    def sum_sent(slot, width):
+        await_bytes(xbuf.at[0, pl.ds(0, ROWS), pl.ds(0, width)], ls_sem.at[slot])
 
     def rs_arrived(n, j):
-        await_bytes(d2s.at[0], rs_recv.at[n - 1, j])
-
-    def add_rows(n, j, terms, i, r, value=None):
+        width = V if isinstance(n, int) and n == 7 else CH
+        await_bytes(xbuf.at[0, pl.ds(0, ROWS), pl.ds(0, width)], rs_recv.at[n - 1, j])
+
+    def add_rows(n, t, terms, r, dst, value=None):
         size = SLICE if value is None else ROWS
-        cols = pl.ds(pl.multiple_of(j * V + i * T, T), T)
+        cols = pl.ds(pl.multiple_of(t * T, T), T)
         rows = pl.ds(r, size)
         v = accbuf[rows, cols] if value is None else value
-        v = v + hub[2 + lax.rem(n, 2), rows, cols].astype(F32)
+        if n is not None:
+            v = v + hub[2 + lax.rem(n, 2), rows, cols].astype(F32)
         for ref, r0 in terms:
             v = v + ref[pl.ds(r0 + r, size), cols].astype(F32)
-        if isinstance(n, int) and n == 8:
-            y[rows, cols] = v.astype(BF16)
-        else:
-            ls[lax.rem(3 * (n - 1) + j, LS), rows, pl.ds(i * T, T)] = v.astype(BF16)
-
-    def add(n, j, terms, i, value=None):
-        for r in range(0, ROWS, SLICE if value is None else ROWS):
-            add_rows(n, j, terms, i, r, value)
+        dst(rows, v)
 
     terms_c = ((xbuf.at[0], 0), (xbuf.at[1], ROWS))
-    terms_0 = ((xbuf.at[0], ROWS), (xbuf.at[1], 0), (rlate, 0))
+    terms_0 = ((hub.at[5], 0), (xbuf.at[1], 0), (y, 0))
 
     def r_load(i, src, dst, col=0, width=D):
         cols = pl.ds(col, width)
@@ -252,8 +251,8 @@
         return local(rbuf.at[src - 1, :, cols], xbuf.at[h, pl.ds(r, ROWS), cols], r_sem.at[i])
 
     late_loads = (
-        r_load(0, 3, (0, 0)), *(r_load(1 + k, 6, (1, ROWS), k * V, V) for k in range(3)),
-        r_load(4, 1, (0, ROWS)), r_load(5, 5, (1, 0)),
+        r_load(0, 3, (0, 0)), *(r_load(1 + k, 6, (1, ROWS), k * CH, CH) for k in range(2)),
+        local(rbuf.at[0], hub.at[5], r_sem.at[3]), r_load(4, 5, (1, 0)),
     )
 
     def first_tile(i):
@@ -271,7 +270,7 @@
     barrier = pltpu.get_barrier_semaphore()
     for d in (*axes, partner):
         pl.semaphore_signal(barrier, inc=1, device_id={"tp": d}, device_id_type=MESH)
-    rsum[...] = jnp.zeros_like(rsum)
+    hub[5] = jnp.zeros_like(hub[5])
     first_tile(1)
     pl.semaphore_wait(barrier, 4)
     for c in range(2):
@@ -390,10 +389,6 @@
                 load_down(2, p + 2)
                 load_one(wg, 0, p + 3)
 
-                @_when(n > 1)
-                def _():
-                    sum_on(n - 1, 2)
-
                 _when(n == 1)(lambda: third_hop(1))
 
                 for m, role in ((1, B), (3, C)):
@@ -408,14 +403,16 @@
                 for m, src in ((5, 2), (6, 4)):
                     @_when(n == m)
                     def _():
-                        for i in range(3):
+                        for i in range(2):
                             rs_arrived(src, i)
-                        local(rbuf.at[src - 1], rsum, r_sem.at[0]).start()
+                        local(rbuf.at[src - 1], hub.at[5], r_sem.at[0]).start()
 
             step_b(p, j, slot)
             return 0
 
         lax.fori_loop(0, 3, down, 0)
+
+        xs = lax.rem(n + 1, 2)
 
         def gate_up(j, _):
             p = base + 3 + 2 * j
@@ -431,7 +428,7 @@
 
                 @pl.when(n > 4)
                 def _():
-                    local(rbuf.at[0], rsum, r_sem.at[0]).wait()
+                    local(rbuf.at[0], hub.at[5], r_sem.at[0]).wait()
 
                 _when(n == 1)(lambda: relay(3))
 
@@ -441,33 +438,38 @@
                     for c in range(2):
                         ag_start(5, 6, C, c)
 
-            @_when(j > 0)
-            def _():
-                sum_on(n, j - 1)
-                _when(j == 1)(lambda: load_pair(2, p + 2))
-
-                @_when(j == 2)
-                def _():
-                    for i in range(2):
-                        load_down(i, p + 2 + i)
-
-            @pl.when(3 * (n - 1) + j >= LS)
-            def _():
-                sum_sent(3 * (n - 1) + j)
-
-            d2_arrived(n, j)
+                d2_arrived(n, 0)
+
+            @_when(j == 1)
+            def _():
+                sum_on(n, 0)
+                load_pair(2, p + 2)
+
+            pl.when(n > 1)(lambda: sum_sent(j, CH))
+            d2_arrived(n, j + 1)
 
             def extra(i, r):
                 q = (i * ROWS + r) // SLICE
-                for k in range(6 * q // 5, 6 * (q + 1) // 5):
+                for k in range(9 * q // 5, 9 * (q + 1) // 5):
                     t, row = divmod(k * SLICE, ROWS)
-                    if t < 6:
-                        add_rows(n, j, ((rsum, 0),), t, row)
-
-            step_a(p, lax.rem(n + 1, 2), 1, False, j, extra)
+                    if t < 9:
+
+                        def dst(rows, v, t=t):
+                            hub[out_at(j, rows, t * T, T)] = v.astype(BF16)
+
+                        add_rows(n, 9 * j + t, ((hub.at[5], 0),), row, dst)
+
+            step_a(p, xs, 1, False, j, extra)
             return 0
 
-        lax.fori_loop(0, 3, gate_up, 0)
+        lax.fori_loop(0, 2, gate_up, 0)
+        p = base + 7
+        chunk_wait(p)
+        chunk_wait(p + 1)
+        sum_on(n, 1)
+        for i in range(2):
+            load_down(i, p + 2 + i)
+        step_a(p, xs, 1, False, 2)
         return 0
 
     lax.fori_loop(1, 7, block, 0)
@@ -476,26 +478,31 @@
         for i in range(6):
             store(i, rows_b(hb, h, i, s))
 
+    def c_sums(rows, cols):
+        return xbuf.at[0, pl.ds(ROWS + rows.start, rows.size), cols]
+
     def on_c(j):
-        sum_start(7, j, None, rlate)
+        sum_start(
+            7, j, lambda p: nbr[p][C], lambda rows: c_sums(rows, cols_of(j)), ls_sem.at[LS + j], V, y
+        )
 
     def r_due(k):
         rs_arrived(6, k)
         late_loads[1 + k].start()
 
     tops = (
-        lambda: (sum_on(6, 2), load_down(2, FINAL + 2), chunk_wait(FINAL), d2_sent(0), d2_sent(1),
-                 [rs_arrived(n, k) for n in (1, 3, 5) for k in range(3)], r_due(0),
-                 [late_loads[i].start() for i in (0, 4, 5)]),
+        lambda: (load_down(2, FINAL + 2), chunk_wait(FINAL), d2_sent(0), d2_sent(1),
+                 [rs_arrived(n, k) for n in (1, 3, 5) for k in range(2)], r_due(0),
+                 [late_loads[i].start() for i in (0, 3, 4)]),
         lambda: (d2_start(7, 0, 0), chunk_wait(FINAL + 1)),
-        lambda: (d2_start(7, 1, 1), late_loads[0].wait(), late_loads[1].wait(), d2_arrived(7, 0), sum_sent(18), r_due(1)),
-        lambda: (on_c(0), chunk_wait(FINAL + 2), d2_sent(0)),
-        lambda: (d2_start(7, 2, 0), d2_arrived(7, 1), sum_sent(19), late_loads[2].wait()),
-        lambda: (on_c(1), d2_sent(1), r_due(2)),
-        lambda: (d2_start(8, 0, 1), d2_arrived(7, 2), sum_sent(20), late_loads[3].wait()),
+        lambda: (d2_start(7, 1, 1), late_loads[0].wait(), late_loads[1].wait(), d2_arrived(7, 0)),
+        lambda: (on_c(0), chunk_wait(FINAL + 2), d2_sent(0), r_due(1)),
+        lambda: (d2_start(7, 2, 0), d2_arrived(7, 1), late_loads[2].wait()),
+        lambda: (on_c(1), d2_sent(1)),
+        lambda: (d2_start(8, 0, 1), d2_arrived(7, 2)),
         lambda: d2_sent(0),
         lambda: (d2_start(8, 1, 0), d2_sent(1), on_c(2)),
-        lambda: (d2_start(8, 2, 1), d2_arrived(8, 0), rs_arrived(7, 0), late_loads[4].wait(), late_loads[5].wait()),
+        lambda: (d2_start(8, 2, 1), d2_arrived(8, 0), rs_arrived(7, 0), late_loads[3].wait(), late_loads[4].wait()),
         lambda: (d2_arrived(8, 1), rs_arrived(7, 1)),
     )
 
@@ -522,7 +529,18 @@
         for cond, n, terms in ((w_c, 7, terms_c), (w_0, 8, terms_0)):
             @pl.when(cond)
             def _():
-                group(s, g, 8 - n, 1, lambda i, v: add(n, g, terms, i, v))
+                def store(i, v):
+                    cols = pl.ds(pl.multiple_of(g * V + i * T, T), T)
+
+                    def dst(rows, v):
+                        if n == 7:
+                            xbuf[0, pl.ds(ROWS, ROWS), cols] = v.astype(BF16)
+                        else:
+                            y[rows, cols] = v.astype(BF16)
+
+                    add_rows(n, 6 * g + i, terms, 0, dst, v)
+
+                group(s, g, 8 - n, 1, store)
 
         return 0
 
@@ -533,19 +551,31 @@
 
     def keep(i, v):
         cols = pl.ds(last * V + i * T, T)
-        accbuf[:, cols] = v
+
+        def dst(rows, v):
+            accbuf[rows, cols] = v
+
+        add_rows(8, 6 * last + i, terms_0[:2], 0, dst, v)
 
     group((FINAL + last) % RING, last, 0, 1, keep)
     rs_arrived(7, last)
     for i in range(6):
-        add(8, last, terms_0, i)
+        cols = pl.ds(last * V + i * T, T)
+
+        def dst(rows, v, cols=cols):
+            y[rows, cols] = v.astype(BF16)
+
+        for r in range(0, ROWS, SLICE):
+            add_rows(None, 6 * last + i, terms_0[2:], r, dst)
 
     d2_sent(0)
     d2_sent(1)
     await_bytes(xall.at[:, 0], ag_send.at[0])
     await_bytes(xall.at[pl.ds(0, 4)], ag_send.at[1])
     for s in range(LS):
-        sum_sent(s)
+        sum_sent(s, CH)
+    for s in range(3):
+        sum_sent(LS + s, V)
 
 
 def _call(x, wg, wu, wd):
@@ -561,15 +591,12 @@
         out_specs=[pl.BlockSpec(memory_space=m) for m in (pltpu.VMEM, pltpu.HBM, pltpu.HBM)],
         scratch_shapes=[
             pltpu.VMEM((2, 2 * ROWS, D), BF16),
-            pltpu.VMEM((4, *rows), BF16),
+            pltpu.VMEM((6, *rows), BF16),
             pltpu.VMEM((RING, F, V), BF16),
             pltpu.VMEM(rows, F32),
             pltpu.VMEM((2, ROWS, V), BF16),
-            pltpu.VMEM((LS, ROWS, V), BF16),
-            pltpu.VMEM(rows, BF16),
-            pltpu.VMEM(rows, BF16),
             pltpu.VMEM((2, ROWS, T), F32),
-            *(dma(s) for s in ((RING,), (3,), (2,), (6,), (2,), (7, 2), (8, 2), (2,), (2, 3), (LS,), (7, 3))),
+            *(dma(s) for s in ((RING,), (3,), (2,), (5,), (2,), (7, 2), (8, 2), (2,), (2, 3), (LS + 3,), (7, 3))),
         ],
         compiler_params=pltpu.CompilerParams(
             collective_id=0, has_side_effects=True, vmem_limit_bytes=64_500_000

time: 290 us -> 290 us (level)
  no operation moved by 1% of the time
where the time goes in v6:
time: 290 us
  Pallas kernels  288 us (99%)
    pallas_call x1, Pallas kernels, _call(): pl.pallas_call(_kernel, out_shape=(pltpu.VMEM(rows, BF16), *(pltpu.HBM(sh...  288 us

profile of v6, /device:TPU:0, one launch (start us, length us, event | category | flops | bytes accessed | tf_op | source)
XLA Modules:
  0.0 289.8 jit_solution(701269036979458379)
XLA Ops:
  0.0 288.4 %mlp.1 = (bf16[256,4608]{1,0:T(8,128)(2,1)S(1)}, bf16[7,2,256,4608]{3,2,1,0:T(8,128)(2,1)}, bf16[6,256,4608]{2,1,0:T(8,128)(2,1)}) custom-call(bf16[256,4608]{1,0:T(8,128)(2,1)} %x.1, bf16[4608,2304]{1,0:T(8,128)(2,1)} %wg.1, bf16[4608,2304]{1,0:T(8,128)(2,1)} %wu.1, bf16[2304,4608]{1,0:T(8,128)(2,1)} %wd.1), custom_call_target="tpu_custom_call" | custom-call | tf_op jit(solution)/shard_map/mlp/pallas_call | solution.py:584
  288.4 1.4 copy.6

commit v7 on v6

--- a/solution.py
+++ b/solution.py
@@ -391,14 +391,19 @@
 
                 _when(n == 1)(lambda: third_hop(1))
 
-                for m, role in ((1, B), (3, C)):
+                for m, blk, role in ((2, 5, B), (4, 7, C)):
                     @_when(n == m)
                     def _():
                         for c in range(2):
-                            ag_start(0, m + 4, role, c)
-
-                for m, blk in ((2, 4), (4, 6), (5, 7)):
-                    _when(n == m)(functools.partial(relay, blk))
+                            ag_start(0, blk, role, c)
+
+                _when(n == 2)(lambda: relay(4))
+
+                @_when(n == 3)
+                def _():
+                    relay(5)
+                    for c in range(2):
+                        ag_start(5, 6, C, c)
 
                 for m, src in ((5, 2), (6, 4)):
                     @_when(n == m)
@@ -431,12 +436,6 @@
                     local(rbuf.at[0], hub.at[5], r_sem.at[0]).wait()
 
                 _when(n == 1)(lambda: relay(3))
-
-                @_when(n == 2)
-                def _():
-                    relay(5)
-                    for c in range(2):
-                        ag_start(5, 6, C, c)
 
                 d2_arrived(n, 0)
 
@@ -469,6 +468,10 @@
         sum_on(n, 1)
         for i in range(2):
             load_down(i, p + 2 + i)
+
+        for m, blk in ((4, 6), (5, 7)):
+            _when(n == m)(functools.partial(relay, blk))
+
         step_a(p, xs, 1, False, 2)
         return 0
 

time: 290 us -> 288 us (level)
  no operation moved by 1% of the time
where the time goes in v7:
time: 288 us
  Pallas kernels  287 us (100%)
    pallas_call x1, Pallas kernels, _call(): pl.pallas_call(_kernel, out_shape=(pltpu.VMEM(rows, BF16), *(pltpu.HBM(sh...  287 us

profile of v7, /device:TPU:0, one launch (start us, length us, event | category | flops | bytes accessed | tf_op | source)
XLA Modules:
  0.0 288.3 jit_solution(8097741737818577392)
XLA Ops:
  0.0 286.8 %mlp.1 = (bf16[256,4608]{1,0:T(8,128)(2,1)S(1)}, bf16[7,2,256,4608]{3,2,1,0:T(8,128)(2,1)}, bf16[6,256,4608]{2,1,0:T(8,128)(2,1)}) custom-call(bf16[256,4608]{1,0:T(8,128)(2,1)} %x.1, bf16[4608,2304]{1,0:T(8,128)(2,1)} %wg.1, bf16[4608,2304]{1,0:T(8,128)(2,1)} %wu.1, bf16[2304,4608]{1,0:T(8,128)(2,1)} %wd.1), custom_call_target="tpu_custom_call" | custom-call | tf_op jit(solution)/shard_map/mlp/pallas_call | solution.py:587
  286.8 1.4 copy.6
